TPU v7x, 32 devices: a whole 2x2x4 slice. The times are simulated.
32 devices in a mesh: seq: 4 (over z), tensor: 2 (over y), fsdp: 4 (over x, core).
Axes of the slice: x: 2, y: 2, z: 4, core: 2. Of those that a mesh axis runs over, the one named last changes fastest.
Arguments:
- hidden_in: bfloat16 [2048, 2048], P(('seq', 'fsdp'), 'tensor'), may hold values from -12 to 12
- out_cotangent: bfloat16 [2048, 2048], P(('seq', 'fsdp'), 'tensor'), may hold values from -6 to 6
- attn_norm_gain: float32 [2048], replicated, may hold values from 0.1 to 1.9
- attn_norm_bias: float32 [2048], replicated, may hold values from -3 to 3
- mlp_norm_gain: float32 [2048], replicated, may hold values from 0.1 to 1.9
- mlp_norm_bias: float32 [2048], replicated, may hold values from -3 to 3
- qkv_weight: bfloat16 [2048, 6144], P(('seq', 'fsdp'), 'tensor')
- qkv_bias: float32 [6144], P('tensor'), may hold values from -0.6 to 0.6
- proj_weight: bfloat16 [2048, 2048], P(('seq', 'fsdp'), 'tensor'), may hold values from -1.5 to 1.5
- proj_bias: float32 [2048], P('tensor'), may hold values from -3 to 3
- up_weight: bfloat16 [2048, 8192], P(('seq', 'fsdp'), 'tensor'), may hold values from -0.125 to 0.125
- up_bias: float32 [8192], P('tensor'), may hold values from -3 to 3
- down_weight: bfloat16 [2048, 8192], P(('seq', 'fsdp'), 'tensor'), may hold values from -0.0625 to 0.0625
- down_bias: float32 [2048], P('tensor'), may hold values from -3 to 3
Outputs:
- hidden_out: bfloat16 [2048, 2048], P(('seq', 'fsdp'), 'tensor')
- input_grad: bfloat16 [2048, 2048], P(('seq', 'fsdp'), 'tensor')
- attn_gain_grad: float32 [2048], replicated
- attn_bias_grad: float32 [2048], replicated
- mlp_gain_grad: float32 [2048], replicated
- mlp_bias_grad: float32 [2048], replicated
- qkv_weight_grad: float32 [2048, 6144], P(('seq', 'fsdp'), 'tensor')
- qkv_bias_grad: float32 [6144], P('tensor')
- proj_weight_grad: float32 [2048, 2048], P(('seq', 'fsdp'), 'tensor')
- proj_bias_grad: float32 [2048], P('tensor')
- up_weight_grad: float32 [2048, 8192], P(('seq', 'fsdp'), 'tensor')
- up_bias_grad: float32 [8192], P('tensor')
- down_weight_grad: float32 [2048, 8192], P(('seq', 'fsdp'), 'tensor')
- down_bias_grad: float32 [2048], P('tensor')
All inputs are finite; a program needn't handle non-finite values.
Results may differ from a plain program's by a relative error of at most 0.013.
Values may be sent and summed in bfloat16 or wider, within the bound.
A program may use at most 256 MiB of HBM per device.

v0:
```python
import functools
import types

import jax
import jax.numpy as jnp
import numpy as np
from jax import lax
from jax.experimental import pallas as pl
from jax.experimental.pallas import tpu as pltpu
from jax.sharding import PartitionSpec as P

HEAD_DIM = 256
ROT = 64
LANES = 128
STRIP = 256
MESH = pl.DeviceIdType.MESH
VMEM_BYTES = 67_043_328
SMALL, WIDE = jnp.bfloat16, jnp.float32

norm_eps = 1e-05
rope_base = 10000.0

WQ, WP, WU1, WU2, WD1, WD2 = range(6)
P1, D1, D2, Q1, U1, U2 = range(6)


def bits_of(size):
    return [1 << b for b in range(size.bit_length() - 1)]


def bf(value):
    return value.astype(jnp.bfloat16)


def f32(value):
    return value.astype(jnp.float32)


def mm(left, right, left_dim, right_dim):
    return lax.dot_general(
        left, right, (((left_dim,), (right_dim,)), ((), ())), preferred_element_type=jnp.float32
    )


def rotary_tables(tok, blocks):
    half = ROT // 2
    frequency = rope_base ** (-np.arange(half, dtype=np.float64) * 2.0 / ROT)
    lanes = np.zeros(LANES)
    lanes[:half] = frequency
    lanes[half:ROT] = frequency
    inner = np.arange(tok, dtype=np.float64)[:, None] * lanes
    outer = np.arange(blocks, dtype=np.float64)[:, None] * tok * lanes
    pack = lambda a: np.stack([np.cos(a), np.sin(a)]).astype(np.float32)
    return (jnp.asarray(pack(inner)), jnp.asarray(pack(outer)))


def flip(rank, mask, size):
    out = jnp.int32(0)
    for b in range(size.bit_length() - 1):
        digit = lax.rem(lax.div(rank, jnp.int32(1 << b)), jnp.int32(2))
        out = out + ((1 - digit) if mask >> b & 1 else digit) * (1 << b)
    return out


def low_bit(j, size):
    return j & -j if j else size


def line_mask(j):
    mask = 0
    b = 0
    while j >> b:
        if j >> b & 1:
            mask ^= (2 << b) - 1
        b += 1
    return mask


def arrivals(size):
    return sorted(range(1, size), key=lambda j: (-low_bit(j, size), j))


def slot_of(j, bit, size):
    index = 0
    for jj in range(size):
        for bb in bits_of(size):
            if bb < low_bit(jj, size):
                if (jj, bb) == (j, bit):
                    return index
                index += 1
    raise ValueError


def at(index, size):
    return pl.ds(pl.multiple_of(index * size, size), size)


def remote(src, dst, send, recv, peer):
    return pltpu.make_async_remote_copy(
        src_ref=src, dst_ref=dst, send_sem=send, recv_sem=recv, device_id=peer, device_id_type=MESH
    )


def repeat(count, body):
    def step(i, carry):
        body(i)
        return carry

    lax.fori_loop(0, count, step, 0)


def turn(value, cos_part, sin_part):
    half = ROT // 2
    head = value[:, :LANES]
    lane = lax.broadcasted_iota(jnp.int32, head.shape, 1)
    other = jnp.where(
        lane < half, -pltpu.roll(head, LANES - half, 1), pltpu.roll(head, half, 1)
    )
    return jnp.concatenate([head * cos_part + other * sin_part, value[:, LANES:]], axis=1)


def make_core(S, T, F):
    c = types.SimpleNamespace(S=S, T=T, F=F)
    c.z, c.y, c.f = lax.axis_index("seq"), lax.axis_index("tensor"), lax.axis_index("fsdp")
    c.fbits, c.sbits = bits_of(F), bits_of(S)
    sends, busy = [], {}

    def start(copy, key=None):
        copy.start()
        sends.append(copy)
        if key is not None:
            busy.setdefault(key, []).append(copy)

    def free(key):
        done = busy.pop(key, [])
        for copy in done:
            copy.wait_send()
        sends[:] = [s for s in sends if not any(s is copy for copy in done)]

    def finish():
        for copy in sends:
            copy.wait_send()

    def greet():
        barrier = pltpu.get_barrier_semaphore()
        peers = [{"seq": flip(c.z, k, S)} for k in range(1, S)]
        peers += [{"tensor": flip(c.y, t, T)} for t in range(1, T)]
        peers += [{"fsdp": flip(c.f, b, F)} for b in c.fbits]
        for peer in peers:
            pl.semaphore_signal(barrier, inc=1, device_id=peer, device_id_type=MESH)
        pl.semaphore_wait(barrier, len(peers))

    c.start, c.free, c.finish, c.greet = start, free, finish, greet
    return c


def gather_ops(c, e):
    S, T, F, z, y, f = c.S, c.T, c.F, c.z, c.y, c.f
    tok, width = e.hid_in.shape
    rows = e.wq_in.shape[0]
    half = e.wu.shape[1] // 2
    tokens = ((e.hid_in, e.hid), (e.cot_in, e.cot))
    weights = (
        (e.wq_in, e.wq, 0, e.wq.shape[1]),
        (e.wp_in, e.wp, 0, e.wp.shape[1]),
        (e.wu_in, e.wu, 0, half),
        (e.wu_in, e.wu, half, half),
        (e.wd_in, e.wd, 0, half),
        (e.wd_in, e.wd, half, half),
    )
    g = types.SimpleNamespace()

    def tok_sem(a, j, t):
        return (a * S + j) * T + t

    def tok_place(a, j, t):
        return tokens[a][1].at[at(flip(z, line_mask(j), S), tok), at(flip(y, t, T), width)]

    def tok_seq(a, j):
        src = tokens[a][0] if j == 0 else tok_place(a, j, 0)
        dst = tok_place(a, j, 0)
        for b in reversed(c.sbits):
            if b < low_bit(j, S):
                i = tok_sem(a, j + b, 0)
                peer = {"seq": flip(z, line_mask(b), S)}
                c.start(remote(src, dst, e.tok_send.at[i], e.tok_recv.at[i], peer))

    def tok_tensor(a, j):
        src = tokens[a][0] if j == 0 else tok_place(a, j, 0)
        dst = tok_place(a, j, 0)
        for t in range(1, T):
            i = tok_sem(a, j, t)
            peer = {"tensor": flip(y, t, T)}
            c.start(remote(src, dst, e.tok_send.at[i], e.tok_recv.at[i], peer))

    def tok_wait(a, j, t):
        i = tok_sem(a, j, t)
        spot = tok_place(a, j, t)
        peer = {"tensor": flip(y, 1, T)}
        remote(spot, spot, e.tok_send.at[i], e.tok_recv.at[i], peer).wait_recv()

    def tok_own(a):
        return pltpu.make_async_copy(tokens[a][0], tok_place(a, 0, 0), e.own_sem.at[a])

    def tok_direct(a):
        for j in c.sbits:
            tok_wait(a, j, 0)
            tok_seq(a, j)
            tok_tensor(a, j)

    def tok_passed(a):
        for j in arrivals(S):
            if j not in c.sbits:
                tok_wait(a, j, 0)
                tok_seq(a, j)
                tok_tensor(a, j)

    def tok_rest(a):
        tok_own(a).wait()
        for j in range(S):
            for t in range(1, T):
                tok_wait(a, j, t)

    def row_sem(m, k, j):
        return (m * S + k) * F + j

    def row_place(m, k, j):
        _, dst, first, size = weights[m]
        return dst.at[at(flip(z, k, S) * F + flip(f, j, F), rows), first : first + size]

    def row_source(m, zd):
        src, dst, first, size = weights[m]
        return src.at[:, pl.ds(pl.multiple_of(zd * dst.shape[1] + first, LANES), size)]

    def row_seq(m):
        for k in range(1, S):
            i = row_sem(m, k, 0)
            zd = flip(z, k, S)
            src = row_source(m, zd)
            dst = row_place(m, 0, 0)
            c.start(remote(src, dst, e.row_send.at[i], e.row_recv.at[i], {"seq": zd}))

    def row_forward(m, k, j):
        dst = row_place(m, k, j)
        src = row_source(m, z) if k == 0 and j == 0 else dst
        for b in reversed(c.fbits):
            if b < low_bit(j, F):
                i = row_sem(m, k, j + b)
                peer = {"fsdp": flip(f, b, F)}
                c.start(remote(src, dst, e.row_send.at[i], e.row_recv.at[i], peer))

    def row_wait(m, k, j):
        i = row_sem(m, k, j)
        spot = row_place(m, k, j)
        peer = {"seq": flip(z, 1, S)}
        remote(spot, spot, e.row_send.at[i], e.row_recv.at[i], peer).wait_recv()

    def row_own(m):
        return pltpu.make_async_copy(row_source(m, z), row_place(m, 0, 0), e.own_sem.at[2 + m])

    def row_arrive(m):
        for k in range(1, S):
            row_wait(m, k, 0)
            row_forward(m, k, 0)

    def row_relay(m):
        for j in arrivals(F):
            if low_bit(j, F) > 1:
                for k in range(S):
                    row_wait(m, k, j)
                    row_forward(m, k, j)

    def row_rest(m):
        row_own(m).wait()
        for j in arrivals(F):
            if low_bit(j, F) == 1:
                for k in range(S):
                    row_wait(m, k, j)

    def begin_own():
        for a in range(2):
            tok_own(a).start()
        for m in range(6):
            row_own(m).start()

    g.tok_seq, g.tok_tensor, g.tok_direct, g.tok_passed = tok_seq, tok_tensor, tok_direct, tok_passed
    g.tok_rest, g.row_seq, g.row_forward, g.row_arrive = tok_rest, row_seq, row_forward, row_arrive
    g.row_relay, g.row_rest, g.begin_own = row_relay, row_rest, begin_own
    return g


def attention_ops(c, e):
    S, T, F, z, y, f = c.S, c.T, c.F, c.z, c.y, c.f
    tok = e.hid_in.shape[0]
    ntok = e.hid.shape[0]
    keys = e.pair.shape[0]
    scale = HEAD_DIM ** (-0.5)
    chunk = 32
    qc = max(32, min(tok, tok * 1024 // keys))
    o = types.SimpleNamespace()

    def norm():
        def norm_chunk(i):
            part = at(i, chunk)
            x = f32(e.hid[part, :])
            mean = jnp.mean(x, axis=-1, keepdims=True)
            centered = x - mean
            inv_std = lax.rsqrt(jnp.mean(centered * centered, axis=-1, keepdims=True) + norm_eps)
            xhat = centered * inv_std
            e.attn_in[part, :] = bf(xhat * e.attn_gain[...] + e.attn_bias[...])
            e.mlp_in[part, :] = bf(xhat * e.mlp_gain[...] + e.mlp_bias[...])
            e.stat[0, part, :] = jnp.broadcast_to(mean, (chunk, LANES))
            e.stat[1, part, :] = jnp.broadcast_to(inv_std, (chunk, LANES))

        repeat(ntok // chunk, norm_chunk)

    def angles(zd, here=slice(None)):
        block = pl.ds(zd * F + f, 1)
        cos_in, sin_in = e.inner[0, here, :], e.inner[1, here, :]
        cos_out, sin_out = e.outer[0, block, :], e.outer[1, block, :]
        return (cos_in * cos_out - sin_in * sin_out, sin_in * cos_out + cos_in * sin_out)

    def qkv():
        bias = e.qkv_bias[:, at(z, 3 * HEAD_DIM)]
        for n in range(3):
            columns = slice(n * HEAD_DIM, (n + 1) * HEAD_DIM)
            part = mm(e.attn_in[...], e.wq[:, columns], 1, 0) + bias[:, columns]
            for zd in range(S):
                piece = part[zd * tok : (zd + 1) * tok]
                if n < 2:
                    piece = turn(piece, *angles(zd))
                if n == 0:
                    e.query[zd * tok : (zd + 1) * tok, :] = bf(piece)
                else:
                    spot = at(zd * F + f, tok)
                    e.pair[spot, (n - 1) * HEAD_DIM : n * HEAD_DIM] = bf(piece)

    def pair_place(zd, j):
        return e.pair.at[at(zd * F + flip(f, j, F), tok), :]

    def pair_forward(zd, j):
        spot = pair_place(zd, j)
        for b in reversed(c.fbits):
            if b < low_bit(j, F):
                i = zd * F + j + b
                peer = {"fsdp": flip(f, b, F)}
                c.start(remote(spot, spot, e.pair_send.at[i], e.pair_recv.at[i], peer), "pair")

    def pair_wait(zd, j):
        i = zd * F + j
        spot = pair_place(zd, j)
        peer = {"fsdp": flip(f, 1, F)}
        remote(spot, spot, e.pair_send.at[i], e.pair_recv.at[i], peer).wait_recv()

    def pair_own():
        for zd in range(S):
            pair_forward(zd, 0)

    def pair_relay():
        for j in arrivals(F):
            if low_bit(j, F) > 1:
                for zd in range(S):
                    pair_wait(zd, j)
                    pair_forward(zd, j)

    def pair_rest():
        for j in arrivals(F):
            if low_bit(j, F) == 1:
                for zd in range(S):
                    pair_wait(zd, j)

    def masked_scores(zd, i, n):
        start_row = zd * tok + i * qc
        q = e.query[pl.ds(pl.multiple_of(start_row, qc), qc), :]
        scores = mm(q, e.pair[:n, :HEAD_DIM], 1, 1) * scale
        last = (zd * F + f) * tok + i * qc
        ahead = lax.broadcasted_iota(jnp.int32, scores.shape, 1) - lax.broadcasted_iota(
            jnp.int32, scores.shape, 0
        )
        return (scores, ahead <= last)

    def forward():
        for zd in range(S):
            n = (zd + 1) * F * tok

            def forward_chunk(i, zd=zd, n=n):
                here = pl.ds(pl.multiple_of(zd * tok + i * qc, qc), qc)
                scores, allowed = masked_scores(zd, i, n)
                top = jnp.max(jnp.where(allowed, scores, -1e30), axis=-1, keepdims=True)
                terms = jnp.where(allowed, jnp.exp(scores - top), 0.0)
                total = jnp.sum(terms, axis=-1, keepdims=True)
                mixed = mm(bf(terms), e.pair[:n, HEAD_DIM:], 1, 0) / total
                e.attn[here, :] = bf(mixed)
                e.row_info[here, :] = jnp.broadcast_to(top + jnp.log(total), (qc, LANES))

            repeat(tok // qc, forward_chunk)

    def backward():
        e.attn_grad[...] = bf(mm(e.cot[...], e.wp[...], 1, 0))
        for zd in range(S):
            n = (zd + 1) * F * tok

            def backward_chunk(i, zd=zd, n=n):
                here = pl.ds(pl.multiple_of(zd * tok + i * qc, qc), qc)
                scores, allowed = masked_scores(zd, i, n)
                weights_here = jnp.where(allowed, jnp.exp(scores - e.row_info[here, :1]), 0.0)
                grad = e.attn_grad[here, :]
                delta = jnp.sum(f32(grad) * f32(e.attn[here, :]), axis=-1, keepdims=True)
                slopes = mm(grad, e.pair[:n, HEAD_DIM:], 1, 1)
                inner_grad = bf(weights_here * (slopes - delta))
                e.probs[here, :n] = bf(weights_here)
                e.score_grad[here, :n] = inner_grad
                if n < keys:
                    blank = jnp.zeros((qc, keys - n), jnp.bfloat16)
                    e.probs[here, n:] = blank
                    e.score_grad[here, n:] = blank
                cos_part, sin_part = angles(zd, pl.ds(pl.multiple_of(i * qc, qc), qc))
                grad_here = mm(inner_grad, e.pair[:n, :HEAD_DIM], 1, 0) * scale
                e.tg[here, :HEAD_DIM] = bf(turn(grad_here, cos_part, -sin_part))

            repeat(tok // qc, backward_chunk)

    def part_sum(j):
        def lanes(ref):
            return jnp.concatenate(
                [ref[:, at(zd * F + flip(f, j, F), tok)] for zd in range(S)], axis=1
            )

        total = jnp.concatenate(
            [
                mm(lanes(e.score_grad), e.query[...], 0, 0) * scale,
                mm(lanes(e.probs), e.attn_grad[...], 0, 0),
            ],
            axis=1,
        )
        for b in c.fbits:
            if b < low_bit(j, F):
                i = slot_of(j, b, F)
                spot = e.part_in.at[i]
                peer = {"fsdp": flip(f, b, F)}
                remote(spot, spot, e.part_send.at[i], e.part_recv.at[i], peer).wait_recv()
                total = total + f32(e.part_in[i])
        return total

    def part_stage(bit):
        c.free("pair")
        for j in range(1, F):
            if low_bit(j, F) == bit:
                spot = e.pair.at[(j - 1) * ntok : j * ntok, :]
                e.pair[(j - 1) * ntok : j * ntok, :] = bf(part_sum(j))
                i = slot_of(j - bit, bit, F)
                peer = {"fsdp": flip(f, bit, F)}
                here = e.part_in.at[i]
                c.start(remote(spot, here, e.part_send.at[j - 1], e.part_recv.at[i], peer))

    def part_later():
        for bit in c.fbits[1:]:
            part_stage(bit)

    def part_home():
        total = part_sum(0)
        for zd in range(S):
            here = slice(zd * tok, (zd + 1) * tok)
            cos_part, sin_part = angles(zd)
            key_part = turn(total[here, :HEAD_DIM], cos_part, -sin_part)
            e.tg[here, HEAD_DIM : 2 * HEAD_DIM] = bf(key_part)
            e.tg[here, 2 * HEAD_DIM :] = bf(total[here, HEAD_DIM:])

    def up(first, size):
        cols = e.wu.shape[1]
        for n in range(first // STRIP, (first + size) // STRIP):
            strip = slice(n * STRIP, (n + 1) * STRIP)
            bias = e.up_bias[:, pl.ds(pl.multiple_of(z * cols + n * STRIP, STRIP), STRIP)]
            mid = mm(e.mlp_in[...], e.wu[:, strip], 1, 0) + bias
            cdf = 0.5 * (1.0 + lax.erf(mid * 0.7071067811865476))
            e.active[:, strip] = bf(mid * cdf)
            e.slope[:, strip] = cdf + mid * jnp.exp(-0.5 * mid * mid) * 0.3989422804014327

    o.norm, o.qkv, o.pair_own, o.pair_relay, o.pair_rest = norm, qkv, pair_own, pair_relay, pair_rest
    o.forward, o.backward, o.part_stage, o.part_later = forward, backward, part_stage, part_later
    o.part_home, o.up = part_home, up
    return o


def grad_units(ff):
    half = ff // 2
    return (
        (0, 0, HEAD_DIM),
        (1, 0, half),
        (1, half, half),
        (2, 0, 3 * HEAD_DIM),
        (3, 0, half),
        (3, half, half),
    )


def spread_ops(c, e, turned):
    S, T, F, z, y, f = c.S, c.T, c.F, c.z, c.y, c.f
    tok, width = e.homes[0].shape
    ntok, D = e.wide.shape
    ff = e.active.shape[1]
    rows = e.grads[0].shape[0]
    rights, lefts = (e.attn, e.active, e.tg, e.pre), (e.cot, e.cot, e.attn_in, e.mlp_in)
    units = grad_units(ff)
    n_u = len(units)
    p = types.SimpleNamespace()

    def block_sum(u, j):
        g, first, size = units[u]
        right, left = rights[g].at[:, first : first + size], lefts[g]
        fd = flip(f, j, F)
        if turned:
            block = jnp.concatenate([left[at(zd * F + fd, rows), :] for zd in range(S)], axis=0)
            total = mm(block, right[...], 1, 0)
        else:
            block = jnp.concatenate([left[:, at(zd * F + fd, rows)] for zd in range(S)], axis=1)
            total = mm(block, right[...], 0, 0)
        for bit in c.fbits:
            if bit < low_bit(j, F):
                s = slot_of(j, bit, F)
                i = u * (F - 1) + s
                spot = e.in_b[u].at[s]
                peer = {"fsdp": flip(f, bit, F)}
                remote(spot, spot, e.out_sem.at[i], e.in_sem.at[i], peer).wait_recv()
                total = total + f32(e.in_b[u][s])
        return total

    def fsdp_stage(u, bit):
        for j in range(1, F):
            if low_bit(j, F) == bit:
                key, spot = e.out_spot(u, j)
                c.free(key)
                spot[...] = bf(block_sum(u, j))
                there = slot_of(j - bit, bit, F)
                send = e.out_sem.at[u * (F - 1) + j - 1]
                recv = e.in_sem.at[u * (F - 1) + there]
                peer = {"fsdp": flip(f, bit, F)}
                c.start(remote(spot, e.in_b[u].at[there], send, recv, peer), key)

    def first(u):
        fsdp_stage(u, c.fbits[0])

    def later(u):
        for bit in c.fbits[1:]:
            fsdp_stage(u, bit)

    def grad_place(u, zd):
        g, first_col, size = units[u]
        start_col = zd * rights[g].shape[1] + first_col
        return e.grads[g].at[:, pl.ds(pl.multiple_of(start_col, LANES), size)]

    def own_grad(u):
        src = e.seq_b[u].at[at(z, rows), :]
        return pltpu.make_async_copy(src, grad_place(u, z), e.home_sem.at[u])

    def seq(u):
        e.seq_b[u][...] = bf(block_sum(u, 0))
        for k in range(1, S):
            peer = flip(z, k, S)
            src, dst = e.seq_b[u].at[at(peer, rows), :], grad_place(u, z)
            i = u * S + k
            c.start(remote(src, dst, e.seq_send.at[i], e.seq_recv.at[i], {"seq": peer}))
        own_grad(u).start()

    def seq_wait():
        for u in range(n_u):
            for k in range(1, S):
                peer = flip(z, k, S)
                spot = grad_place(u, peer)
                i = u * S + k
                remote(spot, spot, e.seq_send.at[i], e.seq_recv.at[i], {"seq": peer}).wait_recv()
            own_grad(u).wait()

    def half_strips(s, t, term):
        for n in range(width // STRIP):
            there = pl.ds(pl.multiple_of(flip(y, t, T) * width + n * STRIP, STRIP), STRIP)
            here = slice(n * STRIP, (n + 1) * STRIP)
            value = term(there)
            if t:
                for zd in range(S):
                    e.y_out[(t - 1) * S + zd, :, here] = bf(value[zd * tok : (zd + 1) * tok])
            elif s == 0:
                e.own_half[:, here] = value
            else:
                e.wide[:, there] = value

    def y_index(s, t, j):
        return (s * max(T - 1, 1) + t - 1) * S + j

    def tensor_send(s):
        for j in [*sorted(range(1, S), key=lambda j: (low_bit(j, S), j)), 0]:
            zd = flip(z, line_mask(j), S)
            for t in range(1, T):
                i = y_index(s, t, j)
                peer = {"tensor": flip(y, t, T)}
                here = e.y_out.at[(t - 1) * S + zd]
                c.start(remote(here, e.y_in.at[i], e.y_send.at[i], e.y_recv.at[i], peer), "y")

    def token_own(s, zd):
        if s == 0:
            return e.own_half.at[at(zd, tok), :]
        return e.wide.at[at(zd, tok), at(y, width)]

    def token_part(s, j):
        total = token_own(s, flip(z, line_mask(j), S))[...]
        for t in range(1, T):
            i = y_index(s, t, j)
            spot = e.y_in.at[i]
            peer = {"tensor": flip(y, t, T)}
            remote(spot, spot, e.y_send.at[i], e.y_recv.at[i], peer).wait_recv()
            total = total + f32(e.y_in[i])
        for bit in c.sbits:
            if bit < low_bit(j, S):
                i = s * (S - 1) + slot_of(j, bit, S)
                spot = e.z_in.at[i]
                peer = {"seq": flip(z, line_mask(bit), S)}
                remote(spot, spot, e.z_send.at[i], e.z_recv.at[i], peer).wait_recv()
                total = total + f32(e.z_in[i])
        return total

    def token_stage(s, bit):
        for j in range(1, S):
            if low_bit(j, S) == bit:
                i = s * (S - 1) + j - 1
                there = s * (S - 1) + slot_of(j - bit, bit, S)
                c.free(("z", j))
                e.z_out[j - 1] = bf(token_part(s, j))
                peer = {"seq": flip(z, line_mask(bit), S)}
                here = e.z_out.at[j - 1]
                copy = remote(here, e.z_in.at[there], e.z_send.at[i], e.z_recv.at[there], peer)
                c.start(copy, ("z", j))

    def token_first(s):
        token_stage(s, c.sbits[0])

    def token_later(s):
        for bit in c.sbits[1:]:
            token_stage(s, bit)

    def home_copy(s):
        return pltpu.make_async_copy(token_own(s, z), e.homes[s], e.home_sem.at[n_u + s])

    def token_home(s):
        total = token_part(s, 0)
        token_own(s, z)[...] = total
        home_copy(s).start()

    def home_wait():
        for s in range(2):
            home_copy(s).wait()

    n_f = len(c.fbits)
    vec = e.vec

    def vec_copy(b):
        peer = {"fsdp": flip(f, c.fbits[b], F)}
        return remote(vec.at[b], e.vec_in.at[b], e.v_send.at[b], e.v_recv.at[b], peer)

    def vec_start(b):
        c.start(vec_copy(b))

    def vec_sum(b):
        vec_copy(b).wait_recv()
        vec[b + 1] = vec[b] + e.vec_in[b]

    def vec_fsdp():
        for b in range(n_f - 1):
            vec_sum(b)
            vec_start(b + 1)

    def vec_seq_copy(k):
        peer = {"seq": flip(z, k, S)}
        i = n_f + k - 1
        return remote(vec.at[n_f], e.vec_seq.at[k - 1], e.v_send.at[i], e.v_recv.at[i], peer)

    def vec_seq_start():
        vec_sum(n_f - 1)
        for k in range(1, S):
            c.start(vec_seq_copy(k))

    def tree(parts):
        while len(parts) > 1:
            parts = [a + b for a, b in zip(parts[::2], parts[1::2])]
        return parts[0]

    def vec_seq_sum():
        parts = []
        for k in range(S):
            if k:
                vec_seq_copy(k).wait_recv()
            value = vec[n_f] if k == 0 else e.vec_seq[k - 1]
            zd = flip(z, k, S)
            e.qkv_bias_o[:, at(zd, 3 * HEAD_DIM)] = value[4:5, : 3 * HEAD_DIM]
            e.up_bias_o[:, at(zd, ff)] = value[5:6, :ff]
            parts.append(value)
        total = tree(parts)
        e.out_bias_o[...] = total[6:7, :width]
        e.vec_ten[0] = total[:4]
        for t in range(1, T):
            c.start(vec_ten_copy(t))

    def vec_ten_copy(t):
        peer = {"tensor": flip(y, t, T)}
        i = n_f + S - 1 + t - 1
        return remote(e.vec_ten.at[0], e.vec_ten.at[t], e.v_send.at[i], e.v_recv.at[i], peer)

    def vec_ten_sum():
        parts = [e.vec_ten[0]]
        for t in range(1, T):
            vec_ten_copy(t).wait_recv()
            parts.append(e.vec_ten[t])
        e.gain_o[...] = tree(parts)

    def branch():
        def term(column):
            return mm(e.active[...], e.wd[column, :], 1, 1) + mm(e.attn[...], e.wp[column, :], 1, 1)

        for t in range(1, T):
            half_strips(0, t, term)
        tensor_send(0)
        return lambda: half_strips(0, 0, term)

    def hidden_grad():
        vec[0] = jnp.zeros(vec.shape[1:], jnp.float32)
        for n in range(ff // STRIP):
            here = slice(n * STRIP, (n + 1) * STRIP)
            value = mm(e.cot[...], e.wd[:, here], 0 if turned else 1, 0) * e.slope[:, here]
            vec[0, 5:6, here] = jnp.sum(value, axis=0, keepdims=True)
            e.pre[:, here] = bf(value)

    def unit_rows(column):
        mean, inv_std = e.stat[0, :, :1], e.stat[1, :, :1]
        return ((f32(e.hid[:, column]) - mean) * inv_std, inv_std)

    def norm_strips():
        lane_parts = range(0, STRIP, LANES)

        def norm_strip(n):
            here = at(n, STRIP)
            a = mm(e.tg[...], e.wq[here, :], 1, 1)
            m = mm(e.pre[...], e.wu[here, :], 1, 1)
            xhat, _ = unit_rows(here)
            vec[0, 0:1, here] = jnp.sum(a * xhat, axis=0, keepdims=True)
            vec[0, 1:2, here] = jnp.sum(a, axis=0, keepdims=True)
            vec[0, 2:3, here] = jnp.sum(m * xhat, axis=0, keepdims=True)
            vec[0, 3:4, here] = jnp.sum(m, axis=0, keepdims=True)
            both = a * e.attn_gain[:, here] + m * e.mlp_gain[:, here]
            e.wide[:, here] = both
            scaled = both * xhat
            e.sums[0] += sum(both[:, i : i + LANES] for i in lane_parts)
            e.sums[1] += sum(scaled[:, i : i + LANES] for i in lane_parts)

        e.sums[...] = jnp.zeros_like(e.sums)
        repeat(D // STRIP, norm_strip)
        vec[0, 4:5, : 3 * HEAD_DIM] = jnp.sum(f32(e.tg[...]), axis=0, keepdims=True)
        vec[0, 6:7, :width] = jnp.sum(f32(e.own_cot()), axis=0, keepdims=True)
        vec_start(0)
        for i in range(2):
            mean = jnp.sum(e.sums[i], axis=-1, keepdims=True) / D
            e.sums[i] = jnp.broadcast_to(mean, e.sums.shape[1:])

    def input_strips():
        def term(column):
            xhat, inv_std = unit_rows(column)
            return inv_std * (e.wide[:, column] - e.sums[0, :, :1] - xhat * e.sums[1, :, :1])

        c.free("y")
        for t in range(1, T):
            half_strips(1, t, term)
        tensor_send(1)
        return lambda: half_strips(1, 0, term)

    p.first, p.later, p.seq, p.seq_wait = first, later, seq, seq_wait
    p.token_first, p.token_later, p.token_home = token_first, token_later, token_home
    p.home_wait, p.vec_fsdp = home_wait, vec_fsdp
    p.vec_seq_start, p.vec_seq_sum, p.vec_ten_sum = vec_seq_start, vec_seq_sum, vec_ten_sum
    p.branch, p.hidden_grad, p.norm_strips, p.input_strips = (
        branch,
        hidden_grad,
        norm_strips,
        input_strips,
    )
    return p


def gather_buffers(S, T, F, tok, width, rows, ff):
    ntok, D, keys = S * tok, T * width, S * F * tok
    kept = {
        "hid": ((ntok, D), SMALL),
        "cot": ((ntok, D), SMALL),
        "attn_in": ((ntok, D), SMALL),
        "mlp_in": ((ntok, D), SMALL),
        "stat": ((2, ntok, LANES), WIDE),
        "wq": ((D, 3 * HEAD_DIM), SMALL),
        "wp": ((D, HEAD_DIM), SMALL),
        "wu": ((D, ff), SMALL),
        "wd": ((D, ff), SMALL),
        "attn": ((ntok, HEAD_DIM), SMALL),
        "active": ((ntok, ff), SMALL),
        "tg": ((ntok, 3 * HEAD_DIM), SMALL),
    }
    passing = {
        "query": ((ntok, HEAD_DIM), SMALL),
        "pair": ((keys, 2 * HEAD_DIM), SMALL),
        "attn_grad": ((ntok, HEAD_DIM), SMALL),
        "probs": ((ntok, keys), SMALL),
        "score_grad": ((ntok, keys), SMALL),
        "row_info": ((ntok, LANES), WIDE),
        "part_in": ((max(F - 1, 1), ntok, 2 * HEAD_DIM), SMALL),
    }
    sems = {
        "own_sem": 8,
        "tok_send": 2 * S * T,
        "tok_recv": 2 * S * T,
        "row_send": 6 * S * F,
        "row_recv": 6 * S * F,
        "pair_send": S * F,
        "pair_recv": S * F,
        "part_send": max(F - 1, 1),
        "part_recv": max(F - 1, 1),
    }
    return kept, passing, sems


def spread_buffers(S, T, F, tok, width, rows, ff):
    ntok, D = S * tok, T * width
    n_f, n_y, parts = len(bits_of(F)), max(T - 1, 1) * S, max(F - 1, 1)
    held = {
        "pre": ((ntok, ff), SMALL),
        "wide": ((ntok, D), WIDE),
        "own_half": ((ntok, width), WIDE),
        "sums": ((2, ntok, LANES), WIDE),
        "vec": ((n_f + 1, 8, D), WIDE),
        "vec_in": ((n_f, 8, D), WIDE),
        "vec_seq": ((max(S - 1, 1), 8, D), WIDE),
        "vec_ten": ((T, 4, D), WIDE),
        "y_out": ((n_y, tok, width), SMALL),
        "y_in": ((2 * n_y, tok, width), SMALL),
        "z_out": ((max(S - 1, 1), tok, width), SMALL),
        "z_in": ((2 * max(S - 1, 1), tok, width), SMALL),
    }
    for u, (_, _, size) in enumerate(grad_units(ff)):
        held[f"in_b{u}"] = ((parts, S * rows, size), SMALL)
        held[f"seq_b{u}"] = ((S * rows, size), SMALL)
    sems = {
        "home_sem": 8,
        "out_sem": 6 * parts,
        "in_sem": 6 * parts,
        "seq_send": 6 * S,
        "seq_recv": 6 * S,
        "y_send": 2 * n_y,
        "y_recv": 2 * n_y,
        "z_send": 2 * max(S - 1, 1),
        "z_recv": 2 * max(S - 1, 1),
        "v_send": n_f + S + T,
        "v_recv": n_f + S + T,
    }
    outs = {f"grad{g}": ((rows, S * n), SMALL) for g, n in enumerate((HEAD_DIM, ff, 3 * HEAD_DIM, ff))}
    outs |= {f"home{s}": ((tok, width), WIDE) for s in range(2)}
    vectors = {
        "gain_o": ((4, D), WIDE),
        "qkv_bias_o": ((1, 3 * width), WIDE),
        "up_bias_o": ((1, S * ff), WIDE),
        "out_bias_o": ((1, width), WIDE),
    }
    return held, sems, outs, vectors


def send_buffers(S, F, rows, ff, units):
    sizes = [size for _, _, size in grad_units(ff)]
    return {f"out_b{u}": ((max(F - 1, 1), S * rows, sizes[u]), SMALL) for u in units}


def gather_lists(e):
    e.in_b = [getattr(e, f"in_b{u}") for u in range(6)]
    e.seq_b = [getattr(e, f"seq_b{u}") for u in range(6)]
    e.grads = [getattr(e, f"grad{g}") for g in range(4)]
    e.homes = [e.home0, e.home1]


def launch(body, sizes, collective, far, near, outs, near_outs, scratch, sems):
    names = [*far, *near, *outs, *near_outs, *scratch, *sems]

    def kernel(*refs):
        body(types.SimpleNamespace(**dict(zip(names, refs))), *sizes)

    kernel.__name__ = body.__name__
    any_spec = pl.BlockSpec(memory_space=pl.ANY)
    vmem = pl.BlockSpec(memory_space=pltpu.VMEM)
    results = pl.pallas_call(
        kernel,
        out_shape=[jax.ShapeDtypeStruct(*o) for o in [*outs.values(), *near_outs.values()]],
        in_specs=[any_spec] * len(far) + [vmem] * len(near),
        out_specs=[any_spec] * len(outs) + [vmem] * len(near_outs),
        scratch_shapes=[pltpu.VMEM(*s) for s in scratch.values()]
        + [pltpu.SemaphoreType.DMA((n,)) for n in sems.values()],
        compiler_params=pltpu.CompilerParams(
            collective_id=collective, has_side_effects=True, vmem_limit_bytes=VMEM_BYTES
        ),
    )(*far.values(), *near.values())
    return dict(zip([*outs, *near_outs], results))


def whole_kernel(e, S, T, F):
    c = make_core(S, T, F)
    width = e.hid_in.shape[1]
    tok = e.hid_in.shape[0]
    ff = e.active.shape[1]
    half = ff // 2
    gather_lists(e)
    e.slope = e.wide.at[:, :ff]
    e.row_info = e.sums.at[0]
    e.own_cot = lambda: e.cot[at(c.z, tok), at(c.y, width)]
    wide_q = 3 * HEAD_DIM
    lent = [e.probs.at[:, :wide_q], e.probs.at[:, wide_q : 2 * wide_q], e.score_grad.at[:, :wide_q]]

    def out_spot(u, j):
        if u == Q1:
            return (("out", u, j), lent[j - 1])
        shared = {U1: D1, U2: D2}.get(u, u)
        return (("out", shared, j), getattr(e, f"out_b{shared}").at[j - 1])

    e.out_spot = out_spot
    g, o, p = gather_ops(c, e), attention_ops(c, e), spread_ops(c, e, False)

    c.greet()
    g.tok_seq(0, 0)
    g.tok_direct(0)
    g.row_seq(WQ)
    g.row_forward(WU2, 0, 0)
    g.row_forward(WQ, 0, 0)
    g.row_arrive(WQ)
    g.begin_own()
    g.row_seq(WU1)
    g.tok_tensor(0, 0)
    g.row_forward(WD2, 0, 0)
    g.row_relay(WQ)
    g.row_rest(WQ)
    g.row_seq(WU2)
    g.tok_passed(0)
    g.row_arrive(WU1)
    g.tok_rest(0)
    g.tok_seq(1, 0)
    g.row_arrive(WU2)
    g.row_forward(WP, 0, 0)
    g.row_forward(WU1, 0, 0)
    g.tok_tensor(1, 0)
    o.norm()
    o.qkv()
    o.pair_own()
    g.row_seq(WP)
    g.tok_direct(1)
    g.row_relay(WU2)
    g.row_rest(WU2)
    g.row_forward(WD1, 0, 0)
    g.row_relay(WU1)
    g.row_arrive(WP)
    g.row_rest(WU1)
    g.row_seq(WD1)
    g.tok_passed(1)
    o.pair_relay()
    o.up(half, half)
    o.up(0, half)
    g.row_arrive(WD1)
    g.row_seq(WD2)
    g.tok_rest(1)
    p.first(D2)
    o.pair_rest()
    g.row_relay(WP)
    p.later(D2)
    g.row_rest(WP)
    o.forward()
    g.row_relay(WD1)
    g.row_arrive(WD2)
    p.first(P1)
    p.first(D1)
    o.backward()
    p.seq(D2)
    o.part_stage(c.fbits[0])
    p.later(P1)
    g.row_rest(WD1)
    g.row_relay(WD2)
    p.later(D1)
    g.row_rest(WD2)
    own_strips = p.branch()
    p.hidden_grad()
    o.part_later()
    p.seq(P1)
    p.first(U2)
    own_strips()
    p.token_first(0)
    p.seq(D1)
    p.later(U2)
    o.part_home()
    p.first(Q1)
    p.token_later(0)
    p.norm_strips()
    p.vec_fsdp()
    p.later(Q1)
    p.seq(U2)
    own_terms = p.input_strips()
    own_terms()
    p.token_first(1)
    p.vec_seq_start()
    p.seq(Q1)
    p.first(U1)
    p.token_later(1)
    p.vec_seq_sum()
    p.token_home(0)
    p.later(U1)
    p.seq(U1)
    p.token_home(1)
    p.vec_ten_sum()
    p.seq_wait()
    p.home_wait()
    c.finish()


KEPT = ("hid", "cot", "attn_in", "mlp_in", "stat", "wq", "wp", "wu", "wd", "attn", "active", "tg")


def first_kernel(e, S, T, F):
    c = make_core(S, T, F)
    half = e.active.shape[1] // 2
    g, o = gather_ops(c, e), attention_ops(c, e)
    names = [*KEPT, "slope"]

    def out_copy(name):
        i = names.index(name)
        return pltpu.make_async_copy(getattr(e, name), getattr(e, name + "_o"), e.put_sem.at[i])

    c.greet()
    g.tok_seq(0, 0)
    g.tok_tensor(0, 0)
    for m in range(6):
        g.row_forward(m, 0, 0)
    g.begin_own()
    g.tok_direct(0)
    g.row_seq(WQ)
    g.tok_passed(0)
    g.row_seq(WU1)
    g.tok_tensor(1, 0)
    g.tok_rest(0)
    o.norm()
    g.row_arrive(WQ)
    g.tok_seq(1, 0)
    g.row_relay(WQ)
    g.row_rest(WQ)
    o.qkv()
    o.pair_own()
    g.row_arrive(WU1)
    for m in (WP, WU2, WD1, WD2):
        g.row_seq(m)
    g.tok_direct(1)
    g.row_relay(WU1)
    o.pair_relay()
    g.tok_passed(1)
    g.row_rest(WU1)
    o.up(0, half)
    g.row_arrive(WP)
    o.pair_rest()
    o.forward()
    g.row_arrive(WU2)
    g.tok_rest(1)
    g.row_relay(WP)
    g.row_rest(WP)
    o.backward()
    o.part_stage(c.fbits[0])
    g.row_relay(WU2)
    g.row_rest(WU2)
    o.up(half, half)
    o.part_later()
    g.row_arrive(WD1)
    g.row_arrive(WD2)
    o.part_home()
    for m in (WD1, WD2):
        g.row_relay(m)
        g.row_rest(m)
    for name in names:
        out_copy(name).start()
    for name in names:
        out_copy(name).wait()
    c.finish()


def second_kernel(e, S, T, F, turned):
    c = make_core(S, T, F)
    gather_lists(e)
    ff = e.active.shape[1]
    e.slope = e.wide.at[:, :ff]
    e.own_cot = lambda: e.own_cot_in[...]
    e.out_spot = lambda u, j: (("out", u, j), getattr(e, f"out_b{u}").at[j - 1])
    e.wd = e.wu = e.wud
    p = spread_ops(c, e, turned)
    names = [*KEPT, "slope"]

    def load(name):
        i = names.index(name)
        return pltpu.make_async_copy(getattr(e, name + "_i"), getattr(e, name), e.load_sem.at[i])

    for name in names:
        if name != "wu":
            load(name).start()
    c.greet()
    for name in names:
        if name != "wu":
            load(name).wait()
    p.first(P1)
    p.first(D1)
    p.first(D2)
    own_strips = p.branch()
    p.later(P1)
    own_strips()
    p.later(D1)
    p.hidden_grad()
    load("wu").start()
    p.seq(P1)
    p.later(D2)
    p.token_first(0)
    p.first(Q1)
    p.first(U1)
    p.first(U2)
    load("wu").wait()
    p.norm_strips()
    p.seq(D1)
    p.later(Q1)
    own_terms = p.input_strips()
    own_terms()
    p.token_later(0)
    p.seq(D2)
    p.later(U1)
    p.vec_fsdp()
    p.seq(Q1)
    p.later(U2)
    p.token_first(1)
    p.token_home(0)
    p.vec_seq_start()
    p.seq(U1)
    p.seq(U2)
    p.token_later(1)
    p.vec_seq_sum()
    p.vec_ten_sum()
    p.token_home(1)
    p.seq_wait()
    p.home_wait()
    c.finish()


def per_device(
    hidden_in,
    out_cotangent,
    attn_norm_gain,
    attn_norm_bias,
    mlp_norm_gain,
    mlp_norm_bias,
    qkv_weight,
    qkv_bias,
    proj_weight,
    proj_bias,
    up_weight,
    up_bias,
    down_weight,
    down_bias,
):
    S, T, F = [lax.axis_size(a) for a in ("seq", "tensor", "fsdp")]
    tok, width = hidden_in.shape
    rows, ff = qkv_weight.shape[0], up_weight.shape[1] // S
    if width != S * HEAD_DIM or S * F * rows != T * width:
        raise ValueError
    shape = (S, T, F, tok, width, rows, ff)
    inner, outer = rotary_tables(tok, S * F)
    far = {
        "hid_in": hidden_in,
        "cot_in": out_cotangent,
        "wq_in": qkv_weight,
        "wp_in": proj_weight,
        "wu_in": up_weight,
        "wd_in": down_weight,
    }
    row = lambda v: v.reshape(1, -1)
    gains = {"attn_gain": row(attn_norm_gain), "mlp_gain": row(mlp_norm_gain)}
    near = gains | {
        "attn_bias": row(attn_norm_bias),
        "mlp_bias": row(mlp_norm_bias),
        "qkv_bias": row(qkv_bias),
        "up_bias": row(up_bias),
        "inner": inner,
        "outer": outer,
    }
    kept, passing, gather_sems = gather_buffers(*shape)
    held, spread_sems, outs, vectors = spread_buffers(*shape)
    if rows % LANES == 0 and F <= 4:
        scratch = kept | passing | held | send_buffers(S, F, rows, ff, (P1, D1, D2))
        del scratch["row_info"]
        sems = gather_sems | spread_sems
        res = launch(whole_kernel, (S, T, F), 0, far, near, outs, vectors, scratch, sems)
    else:
        slope = {"slope": ((S * tok, ff), WIDE)}
        saved = {k + "_o": v for k, v in (kept | slope).items()}
        sems = gather_sems | {"put_sem": len(saved)}
        scratch = kept | slope | passing
        mid = launch(first_kernel, (S, T, F), 0, far, near, saved, {}, scratch, sems)
        turned = rows % LANES != 0
        if turned:
            for k in ("cot_o", "attn_in_o", "mlp_in_o"):
                mid[k] = mid[k].T
        ins = {k[:-2] + "_i": v for k, v in mid.items()}
        scratch = {k: (ins[k + "_i"].shape, t) for k, (_, t) in kept.items() if k not in ("wu", "wd")}
        scratch |= {"wud": kept["wu"]} | held | send_buffers(S, F, rows, ff, range(6))
        near = gains | {"own_cot_in": out_cotangent}
        sems = spread_sems | {"load_sem": len(ins)}
        res = launch(
            second_kernel, (S, T, F, turned), 1, ins, near, outs, vectors, scratch, sems
        )
    hidden_out = bf(f32(hidden_in) + res["home0"] + proj_bias + down_bias)
    input_grad = bf(f32(out_cotangent) + res["home1"])
    out_bias_grad = res["out_bias_o"].reshape(-1)
    norm_grads = res["gain_o"]
    return (
        hidden_out,
        input_grad,
        norm_grads[0],
        norm_grads[1],
        norm_grads[2],
        norm_grads[3],
        f32(res["grad2"]),
        res["qkv_bias_o"].reshape(-1),
        f32(res["grad0"]),
        out_bias_grad,
        f32(res["grad3"]),
        res["up_bias_o"].reshape(-1),
        f32(res["grad1"]),
        out_bias_grad,
    )


def solution(mesh):
    matrix = P(("seq", "fsdp"), "tensor")
    vector = P("tensor")
    return jax.shard_map(
        per_device,
        mesh=mesh,
        in_specs=(
            matrix, matrix, P(), P(), P(), P(),
            matrix, vector, matrix, vector, matrix, vector, matrix, vector,
        ),
        out_specs=(
            matrix, matrix, P(), P(), P(), P(),
            matrix, vector, matrix, vector, matrix, vector, matrix, vector,
        ),
        check_vma=False,
    )
```

profile of v0, /device:TPU:8, one launch (start us, length us, event | category | flops | bytes accessed | tf_op | source)
XLA Modules:
  0.0 236.3 jit_solution(52883587425692717)
XLA Ops:
  0.6 225.0 %shard_map.263 = (bf16[128,1024]{1,0:T(8,128)(2,1)}, bf16[128,4096]{1,0:T(8,128)(2,1)}, bf16[128,3072]{1,0:T(8,128)(2,1)}, bf16[128,4096]{1,0:T(8,128)(2,1)}, f3...) custom-call(bf16[128,1024]{1,0:T(8,128)(2,1)} %refs_0_.1, ...), custom_call_target="tpu_custom_call" | custom-call | tf_op jit(solution)/shard_map/pallas_call | solution.py:890
  225.7 0.0 copy-start.4
  225.7 0.0 copy-start.1
  225.7 2.4 %add_convert_fusion = (bf16[128,1024]{1,0:T(8,128)(2,1)}, bf16[128,1024]{1,0:T(8,128)(2,1)}) fusion(f32[128,1024]{1,0:T(8,128)} %get-tuple-element.25, bf16[128,1024]{1,0:T(8,128)(2,1)} %refs_1_.1, f32[1024]{0:T(1024)} %param.29, f32[1024]{0:T(1024)} %param.25, f32[128,1024]{1,0:T(8,128)} %get-tuple-element.24, bf16[128,1024]{1,0:T(8,128)(2,1)} %refs_0_.1), kind=kLoop, calls=%fused_computation | loop fusion | flops 1048576 | bytes 2105344 | tf_op jit(solution)/shard_map/convert_element_type | solution.py:32
  228.1 0.0 copy-start
  228.1 0.0 copy-done.4
  228.1 0.6 fusion
  228.7 0.0 copy-done.1
  228.7 1.5 convert_element_type.30
  230.2 0.0 copy-start.2
  230.2 0.0 copy-done
  230.2 0.0 copy-start.3
  230.2 1.5 convert_element_type.31
  231.8 0.0 copy-start.6
  231.8 0.0 copy-start.7
  231.8 0.0 copy-start.5
  231.8 0.0 copy-done.2
  231.8 1.3 convert_element_type.28
  233.1 0.0 copy-done.3
  233.1 0.8 convert_element_type.29
  233.9 0.0 copy-done.6
  233.9 0.6 copy.34
  234.5 0.0 copy-done.7
  234.5 0.6 copy.35
  235.1 0.6 copy.36
  235.7 0.0 copy-done.5
  235.7 0.6 copy.37
Async XLA Ops:
  225.7 2.4 %copy-start.4 = (f32[4,2048]{1,0:T(4,128)S(1)}, f32[4,2048]{1,0:T(4,128)}, u32[]{:S(2)}) copy-start(f32[4,2048]{1,0:T(4,128)} %get-tuple-element.26) | copy-start | bytes 98308
  225.7 3.0 %copy-start.1 = (bf16[128,4096]{1,0:T(8,128)(2,1)S(1)}, bf16[128,4096]{1,0:T(8,128)(2,1)}, u32[]{:S(2)}) copy-start(bf16[128,4096]{1,0:T(8,128)(2,1)} %get-tuple-element.31) | copy-start | bytes 3145732
  228.1 2.2 copy-start
  230.2 1.5 copy-start.2
  230.2 2.8 %copy-start.3 = (bf16[128,1024]{1,0:T(8,128)(2,1)S(1)}, bf16[128,1024]{1,0:T(8,128)(2,1)}, u32[]{:S(2)}) copy-start(bf16[128,1024]{1,0:T(8,128)(2,1)} %get-tuple-element.29) | copy-start | bytes 786436
  231.8 2.2 copy-start.6
  231.8 2.8 %copy-start.7 = (f32[1,3072]{1,0:T(1,128)S(1)}, f32[1,3072]{1,0:T(1,128)}, u32[]{:S(2)}) copy-start(f32[1,3072]{1,0:T(1,128)} %get-tuple-element.28) | copy-start | bytes 36868
  231.8 3.9 %copy-start.5 = (f32[1,4096]{1,0:T(1,128)S(1)}, f32[1,4096]{1,0:T(1,128)}, u32[]{:S(2)}) copy-start(f32[1,4096]{1,0:T(1,128)} %get-tuple-element.32) | copy-start | bytes 49156
where the time goes:
time: 238 us; the launch traced here: 236 us
  Pallas kernels  225 us (95%)
  other arithmetic  7.58 us (3%)
  local copies, waits for them, and re-layouts  3.05 us (1%)
    pallas_call x1, Pallas kernels, launch(): pl.pallas_call(kernel, out_shape=[jax.ShapeDtypeStruct(*o) for o in [*out...  225 us
    convert_element_type x4, other arithmetic, f32(): return value.astype(jnp.float32)  5.19 us

commit v1 on v0

--- a/solution.py
+++ b/solution.py
@@ -143,9 +143,9 @@
 
     def greet():
         barrier = pltpu.get_barrier_semaphore()
-        peers = [{"seq": flip(c.z, k, S)} for k in range(1, S)]
-        peers += [{"tensor": flip(c.y, t, T)} for t in range(1, T)]
-        peers += [{"fsdp": flip(c.f, b, F)} for b in c.fbits]
+        peers = [dict(seq=flip(c.z, k, S)) for k in range(1, S)]
+        peers += [dict(tensor=flip(c.y, t, T)) for t in range(1, T)]
+        peers += [dict(fsdp=flip(c.f, b, F)) for b in c.fbits]
         for peer in peers:
             pl.semaphore_signal(barrier, inc=1, device_id=peer, device_id_type=MESH)
         pl.semaphore_wait(barrier, len(peers))
@@ -182,7 +182,7 @@
         for b in reversed(c.sbits):
             if b < low_bit(j, S):
                 i = tok_sem(a, j + b, 0)
-                peer = {"seq": flip(z, line_mask(b), S)}
+                peer = dict(seq=flip(z, line_mask(b), S))
                 c.start(remote(src, dst, e.tok_send.at[i], e.tok_recv.at[i], peer))
 
     def tok_tensor(a, j):
@@ -190,23 +190,22 @@
         dst = tok_place(a, j, 0)
         for t in range(1, T):
             i = tok_sem(a, j, t)
-            peer = {"tensor": flip(y, t, T)}
+            peer = dict(tensor=flip(y, t, T))
             c.start(remote(src, dst, e.tok_send.at[i], e.tok_recv.at[i], peer))
 
     def tok_wait(a, j, t):
         i = tok_sem(a, j, t)
         spot = tok_place(a, j, t)
-        peer = {"tensor": flip(y, 1, T)}
+        peer = dict(tensor=flip(y, 1, T))
         remote(spot, spot, e.tok_send.at[i], e.tok_recv.at[i], peer).wait_recv()
 
     def tok_own(a):
         return pltpu.make_async_copy(tokens[a][0], tok_place(a, 0, 0), e.own_sem.at[a])
 
-    def tok_direct(a):
-        for j in c.sbits:
-            tok_wait(a, j, 0)
-            tok_seq(a, j)
-            tok_tensor(a, j)
+    def tok_direct(a, j):
+        tok_wait(a, j, 0)
+        tok_seq(a, j)
+        tok_tensor(a, j)
 
     def tok_passed(a):
         for j in arrivals(S):
@@ -232,13 +231,13 @@
         src, dst, first, size = weights[m]
         return src.at[:, pl.ds(pl.multiple_of(zd * dst.shape[1] + first, LANES), size)]
 
-    def row_seq(m):
-        for k in range(1, S):
+    def row_seq(m, *peers):
+        for k in peers or range(1, S):
             i = row_sem(m, k, 0)
             zd = flip(z, k, S)
             src = row_source(m, zd)
             dst = row_place(m, 0, 0)
-            c.start(remote(src, dst, e.row_send.at[i], e.row_recv.at[i], {"seq": zd}))
+            c.start(remote(src, dst, e.row_send.at[i], e.row_recv.at[i], dict(seq=zd)))
 
     def row_forward(m, k, j):
         dst = row_place(m, k, j)
@@ -246,20 +245,20 @@
         for b in reversed(c.fbits):
             if b < low_bit(j, F):
                 i = row_sem(m, k, j + b)
-                peer = {"fsdp": flip(f, b, F)}
+                peer = dict(fsdp=flip(f, b, F))
                 c.start(remote(src, dst, e.row_send.at[i], e.row_recv.at[i], peer))
 
     def row_wait(m, k, j):
         i = row_sem(m, k, j)
         spot = row_place(m, k, j)
-        peer = {"seq": flip(z, 1, S)}
+        peer = dict(seq=flip(z, 1, S))
         remote(spot, spot, e.row_send.at[i], e.row_recv.at[i], peer).wait_recv()
 
     def row_own(m):
         return pltpu.make_async_copy(row_source(m, z), row_place(m, 0, 0), e.own_sem.at[2 + m])
 
-    def row_arrive(m):
-        for k in range(1, S):
+    def row_arrive(m, *peers):
+        for k in peers or range(1, S):
             row_wait(m, k, 0)
             row_forward(m, k, 0)
 
@@ -343,13 +342,13 @@
         for b in reversed(c.fbits):
             if b < low_bit(j, F):
                 i = zd * F + j + b
-                peer = {"fsdp": flip(f, b, F)}
+                peer = dict(fsdp=flip(f, b, F))
                 c.start(remote(spot, spot, e.pair_send.at[i], e.pair_recv.at[i], peer), "pair")
 
     def pair_wait(zd, j):
         i = zd * F + j
         spot = pair_place(zd, j)
-        peer = {"fsdp": flip(f, 1, F)}
+        peer = dict(fsdp=flip(f, 1, F))
         remote(spot, spot, e.pair_send.at[i], e.pair_recv.at[i], peer).wait_recv()
 
     def pair_own():
@@ -437,7 +436,7 @@
             if b < low_bit(j, F):
                 i = slot_of(j, b, F)
                 spot = e.part_in.at[i]
-                peer = {"fsdp": flip(f, b, F)}
+                peer = dict(fsdp=flip(f, b, F))
                 remote(spot, spot, e.part_send.at[i], e.part_recv.at[i], peer).wait_recv()
                 total = total + f32(e.part_in[i])
         return total
@@ -449,7 +448,7 @@
                 spot = e.pair.at[(j - 1) * ntok : j * ntok, :]
                 e.pair[(j - 1) * ntok : j * ntok, :] = bf(part_sum(j))
                 i = slot_of(j - bit, bit, F)
-                peer = {"fsdp": flip(f, bit, F)}
+                peer = dict(fsdp=flip(f, bit, F))
                 here = e.part_in.at[i]
                 c.start(remote(spot, here, e.part_send.at[j - 1], e.part_recv.at[i], peer))
 
@@ -520,7 +519,7 @@
                 s = slot_of(j, bit, F)
                 i = u * (F - 1) + s
                 spot = e.in_b[u].at[s]
-                peer = {"fsdp": flip(f, bit, F)}
+                peer = dict(fsdp=flip(f, bit, F))
                 remote(spot, spot, e.out_sem.at[i], e.in_sem.at[i], peer).wait_recv()
                 total = total + f32(e.in_b[u][s])
         return total
@@ -534,7 +533,7 @@
                 there = slot_of(j - bit, bit, F)
                 send = e.out_sem.at[u * (F - 1) + j - 1]
                 recv = e.in_sem.at[u * (F - 1) + there]
-                peer = {"fsdp": flip(f, bit, F)}
+                peer = dict(fsdp=flip(f, bit, F))
                 c.start(remote(spot, e.in_b[u].at[there], send, recv, peer), key)
 
     def first(u):
@@ -555,12 +554,14 @@
 
     def seq(u):
         e.seq_b[u][...] = bf(block_sum(u, 0))
-        for k in range(1, S):
+        own_grad(u).start()
+
+    def seq_send(u, *peers):
+        for k in peers or range(1, S):
             peer = flip(z, k, S)
             src, dst = e.seq_b[u].at[at(peer, rows), :], grad_place(u, z)
             i = u * S + k
-            c.start(remote(src, dst, e.seq_send.at[i], e.seq_recv.at[i], {"seq": peer}))
-        own_grad(u).start()
+            c.start(remote(src, dst, e.seq_send.at[i], e.seq_recv.at[i], dict(seq=peer)))
 
     def seq_wait():
         for u in range(n_u):
@@ -568,7 +569,7 @@
                 peer = flip(z, k, S)
                 spot = grad_place(u, peer)
                 i = u * S + k
-                remote(spot, spot, e.seq_send.at[i], e.seq_recv.at[i], {"seq": peer}).wait_recv()
+                remote(spot, spot, e.seq_send.at[i], e.seq_recv.at[i], dict(seq=peer)).wait_recv()
             own_grad(u).wait()
 
     def half_strips(s, t, term):
@@ -592,7 +593,7 @@
             zd = flip(z, line_mask(j), S)
             for t in range(1, T):
                 i = y_index(s, t, j)
-                peer = {"tensor": flip(y, t, T)}
+                peer = dict(tensor=flip(y, t, T))
                 here = e.y_out.at[(t - 1) * S + zd]
                 c.start(remote(here, e.y_in.at[i], e.y_send.at[i], e.y_recv.at[i], peer), "y")
 
@@ -606,36 +607,32 @@
         for t in range(1, T):
             i = y_index(s, t, j)
             spot = e.y_in.at[i]
-            peer = {"tensor": flip(y, t, T)}
+            peer = dict(tensor=flip(y, t, T))
             remote(spot, spot, e.y_send.at[i], e.y_recv.at[i], peer).wait_recv()
             total = total + f32(e.y_in[i])
         for bit in c.sbits:
             if bit < low_bit(j, S):
                 i = s * (S - 1) + slot_of(j, bit, S)
                 spot = e.z_in.at[i]
-                peer = {"seq": flip(z, line_mask(bit), S)}
+                peer = dict(seq=flip(z, line_mask(bit), S))
                 remote(spot, spot, e.z_send.at[i], e.z_recv.at[i], peer).wait_recv()
                 total = total + f32(e.z_in[i])
         return total
 
-    def token_stage(s, bit):
-        for j in range(1, S):
-            if low_bit(j, S) == bit:
-                i = s * (S - 1) + j - 1
-                there = s * (S - 1) + slot_of(j - bit, bit, S)
-                c.free(("z", j))
-                e.z_out[j - 1] = bf(token_part(s, j))
-                peer = {"seq": flip(z, line_mask(bit), S)}
-                here = e.z_out.at[j - 1]
-                copy = remote(here, e.z_in.at[there], e.z_send.at[i], e.z_recv.at[there], peer)
-                c.start(copy, ("z", j))
-
-    def token_first(s):
-        token_stage(s, c.sbits[0])
-
-    def token_later(s):
-        for bit in c.sbits[1:]:
-            token_stage(s, bit)
+    def token_send(s, j):
+        bit = low_bit(j, S)
+        i = s * (S - 1) + j - 1
+        there = s * (S - 1) + slot_of(j - bit, bit, S)
+        c.free(("z", j))
+        e.z_out[j - 1] = bf(token_part(s, j))
+        peer = dict(seq=flip(z, line_mask(bit), S))
+        here = e.z_out.at[j - 1]
+        copy = remote(here, e.z_in.at[there], e.z_send.at[i], e.z_recv.at[there], peer)
+        c.start(copy, ("z", j))
+
+    def token_sends(s):
+        for j in sorted(range(1, S), key=lambda j: (low_bit(j, S), j)):
+            token_send(s, j)
 
     def home_copy(s):
         return pltpu.make_async_copy(token_own(s, z), e.homes[s], e.home_sem.at[n_u + s])
@@ -653,7 +650,7 @@
     vec = e.vec
 
     def vec_copy(b):
-        peer = {"fsdp": flip(f, c.fbits[b], F)}
+        peer = dict(fsdp=flip(f, c.fbits[b], F))
         return remote(vec.at[b], e.vec_in.at[b], e.v_send.at[b], e.v_recv.at[b], peer)
 
     def vec_start(b):
@@ -669,7 +666,7 @@
             vec_start(b + 1)
 
     def vec_seq_copy(k):
-        peer = {"seq": flip(z, k, S)}
+        peer = dict(seq=flip(z, k, S))
         i = n_f + k - 1
         return remote(vec.at[n_f], e.vec_seq.at[k - 1], e.v_send.at[i], e.v_recv.at[i], peer)
 
@@ -700,7 +697,7 @@
             c.start(vec_ten_copy(t))
 
     def vec_ten_copy(t):
-        peer = {"tensor": flip(y, t, T)}
+        peer = dict(tensor=flip(y, t, T))
         i = n_f + S - 1 + t - 1
         return remote(e.vec_ten.at[0], e.vec_ten.at[t], e.v_send.at[i], e.v_recv.at[i], peer)
 
@@ -770,8 +767,8 @@
         tensor_send(1)
         return lambda: half_strips(1, 0, term)
 
-    p.first, p.later, p.seq, p.seq_wait = first, later, seq, seq_wait
-    p.token_first, p.token_later, p.token_home = token_first, token_later, token_home
+    p.first, p.later, p.seq, p.seq_send, p.seq_wait = first, later, seq, seq_send, seq_wait
+    p.token_send, p.token_sends, p.token_home = token_send, token_sends, token_home
     p.home_wait, p.vec_fsdp = home_wait, vec_fsdp
     p.vec_seq_start, p.vec_seq_sum, p.vec_ten_sum = vec_seq_start, vec_seq_sum, vec_ten_sum
     p.branch, p.hidden_grad, p.norm_strips, p.input_strips = (
@@ -785,84 +782,84 @@
 
 def gather_buffers(S, T, F, tok, width, rows, ff):
     ntok, D, keys = S * tok, T * width, S * F * tok
-    kept = {
-        "hid": ((ntok, D), SMALL),
-        "cot": ((ntok, D), SMALL),
-        "attn_in": ((ntok, D), SMALL),
-        "mlp_in": ((ntok, D), SMALL),
-        "stat": ((2, ntok, LANES), WIDE),
-        "wq": ((D, 3 * HEAD_DIM), SMALL),
-        "wp": ((D, HEAD_DIM), SMALL),
-        "wu": ((D, ff), SMALL),
-        "wd": ((D, ff), SMALL),
-        "attn": ((ntok, HEAD_DIM), SMALL),
-        "active": ((ntok, ff), SMALL),
-        "tg": ((ntok, 3 * HEAD_DIM), SMALL),
-    }
-    passing = {
-        "query": ((ntok, HEAD_DIM), SMALL),
-        "pair": ((keys, 2 * HEAD_DIM), SMALL),
-        "attn_grad": ((ntok, HEAD_DIM), SMALL),
-        "probs": ((ntok, keys), SMALL),
-        "score_grad": ((ntok, keys), SMALL),
-        "row_info": ((ntok, LANES), WIDE),
-        "part_in": ((max(F - 1, 1), ntok, 2 * HEAD_DIM), SMALL),
-    }
-    sems = {
-        "own_sem": 8,
-        "tok_send": 2 * S * T,
-        "tok_recv": 2 * S * T,
-        "row_send": 6 * S * F,
-        "row_recv": 6 * S * F,
-        "pair_send": S * F,
-        "pair_recv": S * F,
-        "part_send": max(F - 1, 1),
-        "part_recv": max(F - 1, 1),
-    }
+    kept = dict(
+        hid=((ntok, D), SMALL),
+        cot=((ntok, D), SMALL),
+        attn_in=((ntok, D), SMALL),
+        mlp_in=((ntok, D), SMALL),
+        stat=((2, ntok, LANES), WIDE),
+        wq=((D, 3 * HEAD_DIM), SMALL),
+        wp=((D, HEAD_DIM), SMALL),
+        wu=((D, ff), SMALL),
+        wd=((D, ff), SMALL),
+        attn=((ntok, HEAD_DIM), SMALL),
+        active=((ntok, ff), SMALL),
+        tg=((ntok, 3 * HEAD_DIM), SMALL),
+    )
+    passing = dict(
+        query=((ntok, HEAD_DIM), SMALL),
+        pair=((keys, 2 * HEAD_DIM), SMALL),
+        attn_grad=((ntok, HEAD_DIM), SMALL),
+        probs=((ntok, keys), SMALL),
+        score_grad=((ntok, keys), SMALL),
+        row_info=((ntok, LANES), WIDE),
+        part_in=((max(F - 1, 1), ntok, 2 * HEAD_DIM), SMALL),
+    )
+    sems = dict(
+        own_sem=8,
+        tok_send=2 * S * T,
+        tok_recv=2 * S * T,
+        row_send=6 * S * F,
+        row_recv=6 * S * F,
+        pair_send=S * F,
+        pair_recv=S * F,
+        part_send=max(F - 1, 1),
+        part_recv=max(F - 1, 1),
+    )
     return kept, passing, sems
 
 
 def spread_buffers(S, T, F, tok, width, rows, ff):
     ntok, D = S * tok, T * width
     n_f, n_y, parts = len(bits_of(F)), max(T - 1, 1) * S, max(F - 1, 1)
-    held = {
-        "pre": ((ntok, ff), SMALL),
-        "wide": ((ntok, D), WIDE),
-        "own_half": ((ntok, width), WIDE),
-        "sums": ((2, ntok, LANES), WIDE),
-        "vec": ((n_f + 1, 8, D), WIDE),
-        "vec_in": ((n_f, 8, D), WIDE),
-        "vec_seq": ((max(S - 1, 1), 8, D), WIDE),
-        "vec_ten": ((T, 4, D), WIDE),
-        "y_out": ((n_y, tok, width), SMALL),
-        "y_in": ((2 * n_y, tok, width), SMALL),
-        "z_out": ((max(S - 1, 1), tok, width), SMALL),
-        "z_in": ((2 * max(S - 1, 1), tok, width), SMALL),
-    }
+    held = dict(
+        pre=((ntok, ff), SMALL),
+        wide=((ntok, D), WIDE),
+        own_half=((ntok, width), WIDE),
+        sums=((2, ntok, LANES), WIDE),
+        vec=((n_f + 1, 8, D), WIDE),
+        vec_in=((n_f, 8, D), WIDE),
+        vec_seq=((max(S - 1, 1), 8, D), WIDE),
+        vec_ten=((T, 4, D), WIDE),
+        y_out=((n_y, tok, width), SMALL),
+        y_in=((2 * n_y, tok, width), SMALL),
+        z_out=((max(S - 1, 1), tok, width), SMALL),
+        z_in=((2 * max(S - 1, 1), tok, width), SMALL),
+    )
     for u, (_, _, size) in enumerate(grad_units(ff)):
         held[f"in_b{u}"] = ((parts, S * rows, size), SMALL)
         held[f"seq_b{u}"] = ((S * rows, size), SMALL)
-    sems = {
-        "home_sem": 8,
-        "out_sem": 6 * parts,
-        "in_sem": 6 * parts,
-        "seq_send": 6 * S,
-        "seq_recv": 6 * S,
-        "y_send": 2 * n_y,
-        "y_recv": 2 * n_y,
-        "z_send": 2 * max(S - 1, 1),
-        "z_recv": 2 * max(S - 1, 1),
-        "v_send": n_f + S + T,
-        "v_recv": n_f + S + T,
-    }
+    sems = dict(
+        home_sem=8,
+        out_sem=6 * parts,
+        in_sem=6 * parts,
+        seq_send=6 * S,
+        seq_recv=6 * S,
+        y_send=2 * n_y,
+        y_recv=2 * n_y,
+        z_send=2 * max(S - 1, 1),
+        z_recv=2 * max(S - 1, 1),
+        v_send=n_f + S + T,
+        v_recv=n_f + S + T,
+    )
     outs = {f"grad{g}": ((rows, S * n), SMALL) for g, n in enumerate((HEAD_DIM, ff, 3 * HEAD_DIM, ff))}
     outs |= {f"home{s}": ((tok, width), WIDE) for s in range(2)}
-    vectors = {
-        "gain_o": ((4, D), WIDE),
-        "qkv_bias_o": ((1, 3 * width), WIDE),
-        "up_bias_o": ((1, S * ff), WIDE),
-        "out_bias_o": ((1, width), WIDE),
-    }
+    vectors = dict(
+        gain_o=((4, D), WIDE),
+        qkv_bias_o=((1, 3 * width), WIDE),
+        up_bias_o=((1, S * ff), WIDE),
+        out_bias_o=((1, width), WIDE),
+    )
     return held, sems, outs, vectors
 
 
@@ -878,11 +875,11 @@
     e.homes = [e.home0, e.home1]
 
 
-def launch(body, sizes, collective, far, near, outs, near_outs, scratch, sems):
+def launch(body, sizes, collective, far, near, outs, near_outs, scratch, sems, **lists):
     names = [*far, *near, *outs, *near_outs, *scratch, *sems]
 
     def kernel(*refs):
-        body(types.SimpleNamespace(**dict(zip(names, refs))), *sizes)
+        body(types.SimpleNamespace(**dict(zip(names, refs)), **lists), *sizes)
 
     kernel.__name__ = body.__name__
     any_spec = pl.BlockSpec(memory_space=pl.ANY)
@@ -922,108 +919,175 @@
 
     e.out_spot = out_spot
     g, o, p = gather_ops(c, e), attention_ops(c, e), spread_ops(c, e, False)
+    near, vectors = e.near_names, e.vector_names
+
+    def near_copy(i):
+        return pltpu.make_async_copy(getattr(e, near[i] + "_i"), getattr(e, near[i]), e.near_sem.at[i])
+
+    def vec_copy(i):
+        return pltpu.make_async_copy(getattr(e, vectors[i]), getattr(e, vectors[i] + "_h"), e.vec_sem.at[i])
+
+    def begin():
+        g.begin_own()
+        for i in range(len(near)):
+            near_copy(i).start()
+
+    def norm():
+        for i in range(len(near)):
+            near_copy(i).wait()
+        o.norm()
+
+    def vec_home():
+        p.vec_ten_sum()
+        for i in range(len(vectors)):
+            vec_copy(i).start()
 
     c.greet()
+    g.row_seq(WU1, 3)
+    g.row_seq(WU2, 1)
+    g.row_forward(WD2, 0, 0)
+    g.row_forward(WQ, 0, 0)
+    g.row_forward(WP, 0, 0)
+    g.tok_tensor(0, 0)
+    g.row_seq(WP, 1)
+    g.row_seq(WU2, 3)
+    g.row_arrive(WU1, 3)
+    g.row_seq(WQ, 1)
+    g.row_arrive(WU2, 3)
+    g.row_arrive(WU2, 1)
+    g.row_forward(WU2, 0, 0)
+    g.row_seq(WQ, 3)
+    g.row_arrive(WQ, 1)
     g.tok_seq(0, 0)
-    g.tok_direct(0)
-    g.row_seq(WQ)
-    g.row_forward(WU2, 0, 0)
-    g.row_forward(WQ, 0, 0)
-    g.row_arrive(WQ)
-    g.begin_own()
-    g.row_seq(WU1)
-    g.tok_tensor(0, 0)
-    g.row_forward(WD2, 0, 0)
+    begin()
+    g.tok_direct(0, 1)
+    g.row_seq(WU1, 2)
+    g.row_seq(WU1, 1)
+    g.row_forward(WU1, 0, 0)
+    g.tok_tensor(1, 0)
+    g.row_arrive(WP, 1)
+    g.row_forward(WD1, 0, 0)
+    g.tok_direct(0, 2)
+    g.row_arrive(WQ, 3)
+    g.row_seq(WP, 2)
+    g.row_seq(WQ, 2)
+    g.row_arrive(WU1, 1)
+    g.tok_passed(0)
+    g.row_seq(WD2, 1)
+    g.row_arrive(WU1, 2)
+    g.tok_seq(1, 0)
+    g.tok_rest(0)
+    g.row_arrive(WQ, 2)
+    g.row_arrive(WP, 2)
+    g.row_arrive(WD2, 1)
+    g.row_seq(WP, 3)
+    norm()
     g.row_relay(WQ)
     g.row_rest(WQ)
-    g.row_seq(WU2)
-    g.tok_passed(0)
-    g.row_arrive(WU1)
-    g.tok_rest(0)
-    g.tok_seq(1, 0)
-    g.row_arrive(WU2)
-    g.row_forward(WP, 0, 0)
-    g.row_forward(WU1, 0, 0)
-    g.tok_tensor(1, 0)
-    o.norm()
+    g.row_relay(WU1)
+    g.row_seq(WU2, 2)
+    g.row_seq(WD1, 1)
+    g.row_rest(WU1)
+    g.row_arrive(WP, 3)
+    g.tok_direct(1, 1)
     o.qkv()
     o.pair_own()
-    g.row_seq(WP)
-    g.tok_direct(1)
+    g.row_seq(WD1, 3)
+    g.tok_direct(1, 2)
+    g.row_arrive(WD1, 1)
+    o.up(0, half)
+    g.row_seq(WD2, 2)
+    g.row_seq(WD2, 3)
+    g.row_arrive(WD1, 3)
+    g.row_arrive(WU2, 2)
+    o.pair_relay()
+    o.pair_rest()
+    g.tok_passed(1)
+    g.row_arrive(WD2, 2)
+    g.row_seq(WD1, 2)
+    o.forward()
+    g.row_arrive(WD2, 3)
+    g.tok_rest(1)
+    p.first(D1)
+    g.row_arrive(WD1, 2)
     g.row_relay(WU2)
-    g.row_rest(WU2)
-    g.row_forward(WD1, 0, 0)
-    g.row_relay(WU1)
-    g.row_arrive(WP)
-    g.row_rest(WU1)
-    g.row_seq(WD1)
-    g.tok_passed(1)
-    o.pair_relay()
-    o.up(half, half)
-    o.up(0, half)
-    g.row_arrive(WD1)
-    g.row_seq(WD2)
-    g.tok_rest(1)
-    p.first(D2)
-    o.pair_rest()
-    g.row_relay(WP)
-    p.later(D2)
-    g.row_rest(WP)
-    o.forward()
-    g.row_relay(WD1)
-    g.row_arrive(WD2)
-    p.first(P1)
-    p.first(D1)
-    o.backward()
-    p.seq(D2)
-    o.part_stage(c.fbits[0])
-    p.later(P1)
-    g.row_rest(WD1)
     g.row_relay(WD2)
     p.later(D1)
+    g.row_rest(WU2)
+    p.first(P1)
+    g.row_relay(WD1)
     g.row_rest(WD2)
+    o.up(half, half)
+    g.row_relay(WP)
+    p.first(D2)
+    g.row_rest(WP)
+    p.later(D2)
+    g.row_rest(WD1)
     own_strips = p.branch()
-    p.hidden_grad()
+    p.later(P1)
+    p.seq(D1)
+    p.seq_send(D1, 3)
+    own_strips()
+    p.seq_send(D1, 2)
+    p.seq_send(D1, 1)
+    o.backward()
+    o.part_stage(c.fbits[0])
+    p.seq(D2)
+    p.seq_send(D2, 3)
+    p.token_send(0, 3)
     o.part_later()
     p.seq(P1)
+    p.seq_send(D2, 2)
+    p.hidden_grad()
+    p.first(U1)
+    p.seq_send(P1, 2)
     p.first(U2)
-    own_strips()
-    p.token_first(0)
-    p.seq(D1)
+    p.token_send(0, 1)
+    p.later(U1)
+    p.seq_send(D2, 1)
+    p.seq_send(P1, 3)
+    p.token_send(0, 2)
+    o.part_home()
+    p.norm_strips()
+    own_terms = p.input_strips()
+    p.first(Q1)
+    p.seq(U1)
+    p.seq_send(U1, 2)
+    p.seq_send(P1, 1)
+    p.vec_fsdp()
+    own_terms()
+    p.vec_seq_start()
     p.later(U2)
-    o.part_home()
-    p.first(Q1)
-    p.token_later(0)
-    p.norm_strips()
-    p.vec_fsdp()
+    p.token_send(1, 3)
     p.later(Q1)
+    p.seq_send(U1, 3)
     p.seq(U2)
-    own_terms = p.input_strips()
-    own_terms()
-    p.token_first(1)
-    p.vec_seq_start()
+    p.seq_send(U2, 2)
+    p.token_send(1, 2)
+    p.token_send(1, 1)
     p.seq(Q1)
-    p.first(U1)
-    p.token_later(1)
+    p.seq_send(Q1, 2)
     p.vec_seq_sum()
     p.token_home(0)
-    p.later(U1)
-    p.seq(U1)
+    p.seq_send(U1, 1)
+    p.seq_send(U2, 1)
+    p.seq_send(Q1, 1)
+    p.seq_send(U2, 3)
+    p.seq_send(Q1, 3)
+    vec_home()
     p.token_home(1)
-    p.vec_ten_sum()
     p.seq_wait()
     p.home_wait()
+    for i in range(len(vectors)):
+        vec_copy(i).wait()
     c.finish()
-
-
-KEPT = ("hid", "cot", "attn_in", "mlp_in", "stat", "wq", "wp", "wu", "wd", "attn", "active", "tg")
 
 
 def first_kernel(e, S, T, F):
     c = make_core(S, T, F)
     half = e.active.shape[1] // 2
     g, o = gather_ops(c, e), attention_ops(c, e)
-    names = [*KEPT, "slope"]
+    names = e.kept_names
 
     def out_copy(name):
         i = names.index(name)
@@ -1035,7 +1099,8 @@
     for m in range(6):
         g.row_forward(m, 0, 0)
     g.begin_own()
-    g.tok_direct(0)
+    for j in c.sbits:
+        g.tok_direct(0, j)
     g.row_seq(WQ)
     g.tok_passed(0)
     g.row_seq(WU1)
@@ -1051,7 +1116,8 @@
     g.row_arrive(WU1)
     for m in (WP, WU2, WD1, WD2):
         g.row_seq(m)
-    g.tok_direct(1)
+    for j in c.sbits:
+        g.tok_direct(1, j)
     g.row_relay(WU1)
     o.pair_relay()
     g.tok_passed(1)
@@ -1092,7 +1158,7 @@
     e.out_spot = lambda u, j: (("out", u, j), getattr(e, f"out_b{u}").at[j - 1])
     e.wd = e.wu = e.wud
     p = spread_ops(c, e, turned)
-    names = [*KEPT, "slope"]
+    names = e.kept_names
 
     def load(name):
         i = names.index(name)
@@ -1115,29 +1181,33 @@
     p.hidden_grad()
     load("wu").start()
     p.seq(P1)
+    p.seq_send(P1)
     p.later(D2)
-    p.token_first(0)
+    p.token_sends(0)
     p.first(Q1)
     p.first(U1)
     p.first(U2)
     load("wu").wait()
     p.norm_strips()
     p.seq(D1)
+    p.seq_send(D1)
     p.later(Q1)
     own_terms = p.input_strips()
     own_terms()
-    p.token_later(0)
+    p.token_home(0)
     p.seq(D2)
+    p.seq_send(D2)
     p.later(U1)
     p.vec_fsdp()
     p.seq(Q1)
+    p.seq_send(Q1)
     p.later(U2)
-    p.token_first(1)
-    p.token_home(0)
     p.vec_seq_start()
+    p.token_sends(1)
     p.seq(U1)
+    p.seq_send(U1)
     p.seq(U2)
-    p.token_later(1)
+    p.seq_send(U2)
     p.vec_seq_sum()
     p.vec_ten_sum()
     p.token_home(1)
@@ -1169,69 +1239,119 @@
         raise ValueError
     shape = (S, T, F, tok, width, rows, ff)
     inner, outer = rotary_tables(tok, S * F)
-    far = {
-        "hid_in": hidden_in,
-        "cot_in": out_cotangent,
-        "wq_in": qkv_weight,
-        "wp_in": proj_weight,
-        "wu_in": up_weight,
-        "wd_in": down_weight,
-    }
+    far = dict(
+        hid_in=hidden_in,
+        cot_in=out_cotangent,
+        wq_in=qkv_weight,
+        wp_in=proj_weight,
+        wu_in=up_weight,
+        wd_in=down_weight,
+    )
     row = lambda v: v.reshape(1, -1)
-    gains = {"attn_gain": row(attn_norm_gain), "mlp_gain": row(mlp_norm_gain)}
-    near = gains | {
-        "attn_bias": row(attn_norm_bias),
-        "mlp_bias": row(mlp_norm_bias),
-        "qkv_bias": row(qkv_bias),
-        "up_bias": row(up_bias),
-        "inner": inner,
-        "outer": outer,
-    }
+    gains = dict(attn_gain=row(attn_norm_gain), mlp_gain=row(mlp_norm_gain))
+    near = gains | dict(
+        attn_bias=row(attn_norm_bias),
+        mlp_bias=row(mlp_norm_bias),
+        qkv_bias=row(qkv_bias),
+        up_bias=row(up_bias),
+        inner=inner,
+        outer=outer,
+    )
     kept, passing, gather_sems = gather_buffers(*shape)
     held, spread_sems, outs, vectors = spread_buffers(*shape)
-    if rows % LANES == 0 and F <= 4:
-        scratch = kept | passing | held | send_buffers(S, F, rows, ff, (P1, D1, D2))
+    if rows % LANES == 0 and (S, T, F) == (4, 2, 4):
+        scratch = kept | passing | held | send_buffers(S, F, rows, ff, (P1, D1, D2)) | vectors
+        scratch |= {k: (v.shape, v.dtype) for k, v in near.items()}
         del scratch["row_info"]
-        sems = gather_sems | spread_sems
-        res = launch(whole_kernel, (S, T, F), 0, far, near, outs, vectors, scratch, sems)
+        sems = gather_sems | spread_sems | dict(near_sem=len(near), vec_sem=len(vectors))
+        far |= {k + "_i": v for k, v in near.items()}
+        outs |= {k + "_h": v for k, v in vectors.items()}
+        lists = dict(near_names=list(near), vector_names=list(vectors))
+        res = launch(whole_kernel, (S, T, F), 0, far, {}, outs, {}, scratch, sems, **lists)
+        res |= {k: res[k + "_h"] for k in vectors}
     else:
-        slope = {"slope": ((S * tok, ff), WIDE)}
+        slope = dict(slope=((S * tok, ff), WIDE))
         saved = {k + "_o": v for k, v in (kept | slope).items()}
-        sems = gather_sems | {"put_sem": len(saved)}
+        sems = gather_sems | dict(put_sem=len(saved))
         scratch = kept | slope | passing
-        mid = launch(first_kernel, (S, T, F), 0, far, near, saved, {}, scratch, sems)
+        lists = dict(kept_names=[*kept, *slope])
+        mid = launch(first_kernel, (S, T, F), 0, far, near, saved, {}, scratch, sems, **lists)
         turned = rows % LANES != 0
         if turned:
             for k in ("cot_o", "attn_in_o", "mlp_in_o"):
                 mid[k] = mid[k].T
         ins = {k[:-2] + "_i": v for k, v in mid.items()}
         scratch = {k: (ins[k + "_i"].shape, t) for k, (_, t) in kept.items() if k not in ("wu", "wd")}
-        scratch |= {"wud": kept["wu"]} | held | send_buffers(S, F, rows, ff, range(6))
-        near = gains | {"own_cot_in": out_cotangent}
-        sems = spread_sems | {"load_sem": len(ins)}
+        scratch |= dict(wud=kept["wu"]) | held | send_buffers(S, F, rows, ff, range(6))
+        near = gains | dict(own_cot_in=out_cotangent)
+        sems = spread_sems | dict(load_sem=len(ins))
         res = launch(
-            second_kernel, (S, T, F, turned), 1, ins, near, outs, vectors, scratch, sems
+            second_kernel, (S, T, F, turned), 1, ins, near, outs, vectors, scratch, sems, **lists
         )
-    hidden_out = bf(f32(hidden_in) + res["home0"] + proj_bias + down_bias)
-    input_grad = bf(f32(out_cotangent) + res["home1"])
-    out_bias_grad = res["out_bias_o"].reshape(-1)
-    norm_grads = res["gain_o"]
-    return (
-        hidden_out,
-        input_grad,
-        norm_grads[0],
-        norm_grads[1],
-        norm_grads[2],
-        norm_grads[3],
-        f32(res["grad2"]),
-        res["qkv_bias_o"].reshape(-1),
-        f32(res["grad0"]),
-        out_bias_grad,
-        f32(res["grad3"]),
-        res["up_bias_o"].reshape(-1),
-        f32(res["grad1"]),
-        out_bias_grad,
-    )
+    return finish(res, hidden_in, out_cotangent, row(proj_bias), row(down_bias))
+
+
+def last_kernel(*refs):
+    sources, (gain, qkv_b, up_b, out_b, proj_bias, down_bias), refs = refs[:8], refs[8:14], refs[14:]
+    outs, refs = refs[:14], refs[14:]
+    held, wide, (hidden, norm, load_sem, out_sem) = refs[:8], refs[8:12], refs[12:]
+    loads = [pltpu.make_async_copy(a, b, load_sem.at[i]) for i, (a, b) in enumerate(zip(sources, held))]
+    for copy in loads:
+        copy.start()
+    stores = []
+
+    def store(src, dst):
+        copy = pltpu.make_async_copy(src, dst, out_sem.at[len(stores)])
+        copy.start()
+        stores.append(copy)
+
+    for i in range(4):
+        store(gain.at[i : i + 1, :], outs[2 + i])
+    for i, ref in enumerate((qkv_b, out_b, up_b, out_b)):
+        store(ref, outs[7 + 2 * i])
+    for i in range(4):
+        loads[i].wait()
+        rows = held[i].shape[0]
+        step = max(16, rows // 4)
+        for r in range(0, rows, step):
+            part = slice(r, r + step)
+            wide[i][part, :] = f32(held[i][part, :])
+            store(wide[i].at[part, :], outs[6 + 2 * i].at[part, :])
+    for copy in loads[4:]:
+        copy.wait()
+    hidden[...] = bf(f32(held[6][...]) + held[4][...] + proj_bias[...] + down_bias[...])
+    norm[...] = bf(f32(held[7][...]) + held[5][...])
+    store(hidden, outs[0])
+    store(norm, outs[1])
+    for copy in stores:
+        copy.wait()
+
+
+def finish(res, hidden_in, out_cotangent, proj_bias, down_bias):
+    r = types.SimpleNamespace(**res)
+    far = [r.grad2, r.grad0, r.grad3, r.grad1, r.home0, r.home1, hidden_in, out_cotangent]
+    near = [r.gain_o, r.qkv_bias_o, r.up_bias_o, r.out_bias_o, proj_bias, down_bias]
+    shape = jax.ShapeDtypeStruct
+    D = r.gain_o.shape[1]
+    qkv_b, up_b, out_b = [shape(v.shape, WIDE) for v in near[1:4]]
+    big = [shape(a.shape, WIDE) for a in far[:4]]
+    outs = [shape(hidden_in.shape, SMALL)] * 2 + [shape((1, D), WIDE)] * 4
+    outs += [big[0], qkv_b, big[1], out_b, big[2], up_b, big[3], out_b]
+    any_spec = pl.BlockSpec(memory_space=pl.ANY)
+    vmem = pl.BlockSpec(memory_space=pltpu.VMEM)
+    results = pl.pallas_call(
+        last_kernel,
+        out_shape=outs,
+        in_specs=[any_spec] * len(far) + [vmem] * len(near),
+        out_specs=[any_spec] * len(outs),
+        scratch_shapes=[pltpu.VMEM(a.shape, a.dtype) for a in far]
+        + [pltpu.VMEM(a.shape, WIDE) for a in far[:4]]
+        + [pltpu.VMEM(hidden_in.shape, SMALL)] * 2
+        + [pltpu.SemaphoreType.DMA((len(far),)), pltpu.SemaphoreType.DMA((32,))],
+        compiler_params=pltpu.CompilerParams(vmem_limit_bytes=VMEM_BYTES),
+    )(*far, *near)
+    flat = {2, 3, 4, 5, 7, 9, 11, 13}
+    return tuple(v.reshape(-1) if i in flat else v for i, v in enumerate(results))
 
 
 def solution(mesh):

time: 238 us -> 224 us (0.941)
  other arithmetic: 7.58 us -> 0 us
  Pallas kernels: 225 us -> 220 us
  local copies, waits for them, and re-layouts: 3.05 us -> 0 us
    pallas_call x1, Pallas kernels: 225 us -> 215 us  [launch(): pl.pallas_call(kernel, out_shape=[jax.ShapeDtypeStruct(*o) for o in [*out...]
    convert_element_type x5 -> x0, other arithmetic: 7.58 us -> none  [the longest x4 5.19 us: f32(): return value.astype(jnp.float32)]
    pallas_call x0 -> x1, Pallas kernels: none -> 5.14 us  [finish(): pl.pallas_call(last_kernel, out_shape=outs, in_specs=[any_spec] * len(far...]
    unnamed x20 -> x0, local copies, waits for them, and re-layouts: 2.43 us -> none
where the time goes in v1:
time: 224 us; the launch traced here: 221 us
  Pallas kernels  220 us (98%)
    pallas_call x1, Pallas kernels, launch(): pl.pallas_call(kernel, out_shape=[jax.ShapeDtypeStruct(*o) for o in [*out...  215 us
    pallas_call x1, Pallas kernels, finish(): pl.pallas_call(last_kernel, out_shape=outs, in_specs=[any_spec] * len(far...  5.14 us

profile of v1, /device:TPU:8, one launch (start us, length us, event | category | flops | bytes accessed | tf_op | source)
XLA Modules:
  0.0 220.7 jit_solution(3087072094295439265)
XLA Ops:
  0.7 214.7 %shard_map.263 = (bf16[128,1024]{1,0:T(8,128)(2,1)}, bf16[128,4096]{1,0:T(8,128)(2,1)}, bf16[128,3072]{1,0:T(8,128)(2,1)}, bf16[128,4096]{1,0:T(8,128)(2,1)}, f3...) custom-call(bf16[128,1024]{1,0:T(8,128)(2,1)} %refs_6_.1, ...), custom_call_target="tpu_custom_call" | custom-call | tf_op jit(solution)/shard_map/pallas_call | solution.py:887
  215.4 5.1 %shard_map.264 = (bf16[128,1024]{1,0:T(8,128)(2,1)}, bf16[128,1024]{1,0:T(8,128)(2,1)}, f32[1,2048]{1,0:T(1,128)}, f32[1,2048]{1,0:T(1,128)}, f32[1,2048]{1,0:T(...) custom-call(bf16[128,3072]{1,0:T(8,128)(2,1)} %get-tuple-element.38., ...), custom_call_target="tpu_custom_call" | custom-call | tf_op jit(solution)/shard_map/pallas_call | solution.py:1342

commit v2 on v1

--- a/solution.py
+++ b/solution.py
@@ -292,10 +292,8 @@
     S, T, F, z, y, f = c.S, c.T, c.F, c.z, c.y, c.f
     tok = e.hid_in.shape[0]
     ntok = e.hid.shape[0]
-    keys = e.pair.shape[0]
     scale = HEAD_DIM ** (-0.5)
     chunk = 32
-    qc = max(32, min(tok, tok * 1024 // keys))
     o = types.SimpleNamespace()
 
     def norm():
@@ -313,9 +311,9 @@
 
         repeat(ntok // chunk, norm_chunk)
 
-    def angles(zd, here=slice(None)):
+    def angles(zd):
         block = pl.ds(zd * F + f, 1)
-        cos_in, sin_in = e.inner[0, here, :], e.inner[1, here, :]
+        cos_in, sin_in = e.inner[0], e.inner[1]
         cos_out, sin_out = e.outer[0, block, :], e.outer[1, block, :]
         return (cos_in * cos_out - sin_in * sin_out, sin_in * cos_out + cos_in * sin_out)
 
@@ -368,56 +366,77 @@
                 for zd in range(S):
                     pair_wait(zd, j)
 
-    def masked_scores(zd, i, n):
-        start_row = zd * tok + i * qc
-        q = e.query[pl.ds(pl.multiple_of(start_row, qc), qc), :]
-        scores = mm(q, e.pair[:n, :HEAD_DIM], 1, 1) * scale
-        last = (zd * F + f) * tok + i * qc
-        ahead = lax.broadcasted_iota(jnp.int32, scores.shape, 1) - lax.broadcasted_iota(
-            jnp.int32, scores.shape, 0
-        )
-        return (scores, ahead <= last)
+    n = F * tok
+
+    def row_chunks(b, body):
+        count = ntok - b * tok
+        size = count // 2 if count > 2 * tok else count
+        while size * n > 2 * tok * 512 and size > 32:
+            size //= 2
+
+        def step(i):
+            first = pl.multiple_of(b * tok + i * size, 32)
+            here = pl.ds(first, size)
+            scores = mm(e.query[here, :], e.pair[b * n : (b + 1) * n, :HEAD_DIM], 1, 1) * scale
+            row = i * size + lax.broadcasted_iota(jnp.int32, scores.shape, 0)
+            column = lax.broadcasted_iota(jnp.int32, scores.shape, 1)
+            body(here, scores, (column - row <= f * tok) | (row >= tok))
+
+        repeat(count // size, step)
+
+    def wide_rows(value):
+        return jnp.broadcast_to(value, (value.shape[0], LANES))
 
     def forward():
-        for zd in range(S):
-            n = (zd + 1) * F * tok
-
-            def forward_chunk(i, zd=zd, n=n):
-                here = pl.ds(pl.multiple_of(zd * tok + i * qc, qc), qc)
-                scores, allowed = masked_scores(zd, i, n)
+        for b in range(S):
+            values = e.pair.at[b * n : (b + 1) * n, HEAD_DIM:]
+
+            def block(here, scores, allowed, b=b, values=values):
                 top = jnp.max(jnp.where(allowed, scores, -1e30), axis=-1, keepdims=True)
+                if b:
+                    old = e.row_info[here, :1]
+                    top = jnp.maximum(top, old)
                 terms = jnp.where(allowed, jnp.exp(scores - top), 0.0)
                 total = jnp.sum(terms, axis=-1, keepdims=True)
-                mixed = mm(bf(terms), e.pair[:n, HEAD_DIM:], 1, 0) / total
-                e.attn[here, :] = bf(mixed)
-                e.row_info[here, :] = jnp.broadcast_to(top + jnp.log(total), (qc, LANES))
-
-            repeat(tok // qc, forward_chunk)
+                mixed = mm(bf(terms), values[...], 1, 0)
+                if b:
+                    rescale = jnp.exp(old - top)
+                    total = total + e.row_sum[here, :1] * rescale
+                    mixed = mixed + e.acc[here, :] * rescale
+                e.row_info[here, :] = wide_rows(top)
+                e.row_sum[here, :] = wide_rows(total)
+                e.acc[here, :] = mixed
+
+            row_chunks(b, block)
+            done = slice(b * tok, (b + 1) * tok)
+            total = e.row_sum[done, :]
+            e.attn[done, :] = bf(e.acc[done, :] / total[:, :1])
+            e.row_info[done, :] = e.row_info[done, :] + jnp.log(total)
 
     def backward():
         e.attn_grad[...] = bf(mm(e.cot[...], e.wp[...], 1, 0))
-        for zd in range(S):
-            n = (zd + 1) * F * tok
-
-            def backward_chunk(i, zd=zd, n=n):
-                here = pl.ds(pl.multiple_of(zd * tok + i * qc, qc), qc)
-                scores, allowed = masked_scores(zd, i, n)
+        delta = jnp.sum(f32(e.attn_grad[...]) * f32(e.attn[...]), axis=-1, keepdims=True)
+        e.row_sum[...] = wide_rows(delta)
+        for b in range(S):
+            keys_here = slice(b * n, (b + 1) * n)
+
+            def block(here, scores, allowed, b=b, keys_here=keys_here):
                 weights_here = jnp.where(allowed, jnp.exp(scores - e.row_info[here, :1]), 0.0)
-                grad = e.attn_grad[here, :]
-                delta = jnp.sum(f32(grad) * f32(e.attn[here, :]), axis=-1, keepdims=True)
-                slopes = mm(grad, e.pair[:n, HEAD_DIM:], 1, 1)
-                inner_grad = bf(weights_here * (slopes - delta))
-                e.probs[here, :n] = bf(weights_here)
-                e.score_grad[here, :n] = inner_grad
-                if n < keys:
-                    blank = jnp.zeros((qc, keys - n), jnp.bfloat16)
-                    e.probs[here, n:] = blank
-                    e.score_grad[here, n:] = blank
-                cos_part, sin_part = angles(zd, pl.ds(pl.multiple_of(i * qc, qc), qc))
-                grad_here = mm(inner_grad, e.pair[:n, :HEAD_DIM], 1, 0) * scale
-                e.tg[here, :HEAD_DIM] = bf(turn(grad_here, cos_part, -sin_part))
-
-            repeat(tok // qc, backward_chunk)
+                slopes = mm(e.attn_grad[here, :], e.pair[keys_here, HEAD_DIM:], 1, 1)
+                inner_grad = bf(weights_here * (slopes - e.row_sum[here, :1]))
+                e.probs[here, keys_here] = bf(weights_here)
+                e.score_grad[here, keys_here] = inner_grad
+                term = mm(inner_grad, e.pair[keys_here, :HEAD_DIM], 1, 0)
+                e.acc[here, :] = e.acc[here, :] + term if b else term
+
+            row_chunks(b, block)
+            if b:
+                blank = jnp.zeros((b * tok, n), jnp.bfloat16)
+                e.probs[: b * tok, keys_here] = blank
+                e.score_grad[: b * tok, keys_here] = blank
+            done = slice(b * tok, (b + 1) * tok)
+            cos_part, sin_part = angles(b)
+            e.tg[done, :HEAD_DIM] = bf(turn(e.acc[done, :] * scale, cos_part, -sin_part))
 
     def part_sum(j):
         def lanes(ref):
@@ -729,32 +748,40 @@
         mean, inv_std = e.stat[0, :, :1], e.stat[1, :, :1]
         return ((f32(e.hid[:, column]) - mean) * inv_std, inv_std)
 
+    def add_strip(here, value, gain, row):
+        xhat, _ = unit_rows(here)
+        scaled = value * xhat
+        vec[0, row : row + 1, here] = jnp.sum(scaled, axis=0, keepdims=True)
+        vec[0, row + 1 : row + 2, here] = jnp.sum(value, axis=0, keepdims=True)
+        gain_here = gain[:, here]
+        both, scaled = value * gain_here, scaled * gain_here
+        lane_parts = range(0, STRIP, LANES)
+        e.sums[0] += sum(both[:, i : i + LANES] for i in lane_parts)
+        e.sums[1] += sum(scaled[:, i : i + LANES] for i in lane_parts)
+        return both
+
+    def mlp_strips():
+        def strip(n):
+            here = at(n, STRIP)
+            e.wide[:, here] = add_strip(here, mm(e.pre[...], e.wu[here, :], 1, 1), e.mlp_gain, 2)
+
+        e.sums[...] = jnp.zeros_like(e.sums)
+        repeat(D // STRIP, strip)
+
     def norm_strips():
-        lane_parts = range(0, STRIP, LANES)
-
-        def norm_strip(n):
+        def strip(n):
             here = at(n, STRIP)
-            a = mm(e.tg[...], e.wq[here, :], 1, 1)
-            m = mm(e.pre[...], e.wu[here, :], 1, 1)
-            xhat, _ = unit_rows(here)
-            vec[0, 0:1, here] = jnp.sum(a * xhat, axis=0, keepdims=True)
-            vec[0, 1:2, here] = jnp.sum(a, axis=0, keepdims=True)
-            vec[0, 2:3, here] = jnp.sum(m * xhat, axis=0, keepdims=True)
-            vec[0, 3:4, here] = jnp.sum(m, axis=0, keepdims=True)
-            both = a * e.attn_gain[:, here] + m * e.mlp_gain[:, here]
-            e.wide[:, here] = both
-            scaled = both * xhat
-            e.sums[0] += sum(both[:, i : i + LANES] for i in lane_parts)
-            e.sums[1] += sum(scaled[:, i : i + LANES] for i in lane_parts)
-
-        e.sums[...] = jnp.zeros_like(e.sums)
-        repeat(D // STRIP, norm_strip)
+            e.wide[:, here] += add_strip(here, mm(e.tg[...], e.wq[here, :], 1, 1), e.attn_gain, 0)
+
+        repeat(D // STRIP, strip)
+        for i in range(2):
+            mean = jnp.sum(e.sums[i], axis=-1, keepdims=True) / D
+            e.sums[i] = jnp.broadcast_to(mean, e.sums.shape[1:])
+
+    def vec_begin():
         vec[0, 4:5, : 3 * HEAD_DIM] = jnp.sum(f32(e.tg[...]), axis=0, keepdims=True)
         vec[0, 6:7, :width] = jnp.sum(f32(e.own_cot()), axis=0, keepdims=True)
         vec_start(0)
-        for i in range(2):
-            mean = jnp.sum(e.sums[i], axis=-1, keepdims=True) / D
-            e.sums[i] = jnp.broadcast_to(mean, e.sums.shape[1:])
 
     def input_strips():
         def term(column):
@@ -771,12 +798,8 @@
     p.token_send, p.token_sends, p.token_home = token_send, token_sends, token_home
     p.home_wait, p.vec_fsdp = home_wait, vec_fsdp
     p.vec_seq_start, p.vec_seq_sum, p.vec_ten_sum = vec_seq_start, vec_seq_sum, vec_ten_sum
-    p.branch, p.hidden_grad, p.norm_strips, p.input_strips = (
-        branch,
-        hidden_grad,
-        norm_strips,
-        input_strips,
-    )
+    p.branch, p.hidden_grad, p.mlp_strips = branch, hidden_grad, mlp_strips
+    p.norm_strips, p.input_strips, p.vec_begin = norm_strips, input_strips, vec_begin
     return p
 
 
@@ -803,6 +826,8 @@
         probs=((ntok, keys), SMALL),
         score_grad=((ntok, keys), SMALL),
         row_info=((ntok, LANES), WIDE),
+        row_sum=((ntok, LANES), WIDE),
+        acc=((ntok, HEAD_DIM), WIDE),
         part_in=((max(F - 1, 1), ntok, 2 * HEAD_DIM), SMALL),
     )
     sems = dict(
@@ -906,7 +931,8 @@
     half = ff // 2
     gather_lists(e)
     e.slope = e.wide.at[:, :ff]
-    e.row_info = e.sums.at[0]
+    e.row_info, e.row_sum = e.sums.at[0], e.sums.at[1]
+    e.acc = e.wide.at[:, ff : ff + HEAD_DIM]
     e.own_cot = lambda: e.cot[at(c.z, tok), at(c.y, width)]
     wide_q = 3 * HEAD_DIM
     lent = [e.probs.at[:, :wide_q], e.probs.at[:, wide_q : 2 * wide_q], e.score_grad.at[:, :wide_q]]
@@ -943,139 +969,141 @@
             vec_copy(i).start()
 
     c.greet()
-    g.row_seq(WU1, 3)
     g.row_seq(WU2, 1)
-    g.row_forward(WD2, 0, 0)
-    g.row_forward(WQ, 0, 0)
-    g.row_forward(WP, 0, 0)
-    g.tok_tensor(0, 0)
-    g.row_seq(WP, 1)
-    g.row_seq(WU2, 3)
-    g.row_arrive(WU1, 3)
-    g.row_seq(WQ, 1)
-    g.row_arrive(WU2, 3)
-    g.row_arrive(WU2, 1)
-    g.row_forward(WU2, 0, 0)
-    g.row_seq(WQ, 3)
-    g.row_arrive(WQ, 1)
+    g.row_forward(WU1, 0, 0)
+    g.tok_tensor(1, 0)
+    g.row_seq(WQ, 2)
     g.tok_seq(0, 0)
     begin()
+    g.tok_tensor(0, 0)
+    g.row_forward(WQ, 0, 0)
+    g.row_seq(WQ, 1)
+    g.row_seq(WQ, 3)
+    g.row_seq(WD2, 1)
+    g.row_forward(WD1, 0, 0)
+    g.row_seq(WP, 3)
+    g.row_arrive(WQ, 1)
+    g.row_seq(WU2, 2)
+    g.row_arrive(WQ, 2)
+    g.row_arrive(WD2, 1)
+    g.tok_direct(0, 2)
+    g.row_forward(WP, 0, 0)
+    g.row_arrive(WQ, 3)
+    g.row_forward(WU2, 0, 0)
+    g.row_seq(WU2, 3)
+    g.row_arrive(WU2, 2)
     g.tok_direct(0, 1)
+    g.row_seq(WP, 2)
+    g.row_relay(WQ)
+    g.row_seq(WU1, 1)
+    g.row_seq(WU1, 3)
+    g.row_seq(WP, 1)
+    g.tok_passed(0)
+    g.row_arrive(WP, 2)
+    g.row_arrive(WU2, 3)
+    g.row_rest(WQ)
+    g.row_arrive(WU2, 1)
+    g.row_forward(WD2, 0, 0)
+    g.tok_seq(1, 0)
+    g.row_arrive(WU1, 1)
+    g.tok_rest(0)
+    norm()
     g.row_seq(WU1, 2)
-    g.row_seq(WU1, 1)
-    g.row_forward(WU1, 0, 0)
-    g.tok_tensor(1, 0)
-    g.row_arrive(WP, 1)
-    g.row_forward(WD1, 0, 0)
-    g.tok_direct(0, 2)
-    g.row_arrive(WQ, 3)
-    g.row_seq(WP, 2)
-    g.row_seq(WQ, 2)
-    g.row_arrive(WU1, 1)
-    g.tok_passed(0)
-    g.row_seq(WD2, 1)
-    g.row_arrive(WU1, 2)
-    g.tok_seq(1, 0)
-    g.tok_rest(0)
-    g.row_arrive(WQ, 2)
-    g.row_arrive(WP, 2)
-    g.row_arrive(WD2, 1)
-    g.row_seq(WP, 3)
-    norm()
-    g.row_relay(WQ)
-    g.row_rest(WQ)
-    g.row_relay(WU1)
-    g.row_seq(WU2, 2)
-    g.row_seq(WD1, 1)
-    g.row_rest(WU1)
+    o.qkv()
+    o.pair_own()
     g.row_arrive(WP, 3)
     g.tok_direct(1, 1)
-    o.qkv()
-    o.pair_own()
+    g.row_relay(WU2)
+    g.tok_direct(1, 2)
+    g.row_rest(WU2)
+    g.row_seq(WD2, 2)
+    o.pair_relay()
     g.row_seq(WD1, 3)
-    g.tok_direct(1, 2)
+    g.row_arrive(WU1, 3)
+    g.row_arrive(WU1, 2)
+    o.up(half, half)
+    g.row_seq(WD1, 1)
+    o.pair_rest()
+    o.forward()
+    g.row_arrive(WP, 1)
+    g.row_arrive(WD2, 2)
+    g.row_seq(WD1, 2)
+    g.row_relay(WU1)
+    g.tok_passed(1)
+    g.row_arrive(WD1, 3)
+    g.row_rest(WU1)
     g.row_arrive(WD1, 1)
     o.up(0, half)
-    g.row_seq(WD2, 2)
+    g.row_relay(WP)
     g.row_seq(WD2, 3)
-    g.row_arrive(WD1, 3)
-    g.row_arrive(WU2, 2)
-    o.pair_relay()
-    o.pair_rest()
-    g.tok_passed(1)
-    g.row_arrive(WD2, 2)
-    g.row_seq(WD1, 2)
-    o.forward()
-    g.row_arrive(WD2, 3)
     g.tok_rest(1)
     p.first(D1)
     g.row_arrive(WD1, 2)
-    g.row_relay(WU2)
+    g.row_rest(WP)
+    p.first(D2)
+    g.row_arrive(WD2, 3)
+    p.later(D1)
+    g.row_relay(WD1)
+    g.row_rest(WD1)
     g.row_relay(WD2)
-    p.later(D1)
-    g.row_rest(WU2)
+    g.row_rest(WD2)
+    p.later(D2)
+    own_strips = p.branch()
+    o.backward()
+    p.seq(D1)
+    p.seq_send(D1, 2)
+    o.part_stage(c.fbits[0])
+    p.seq_send(D1, 3)
+    p.seq_send(D1, 1)
     p.first(P1)
-    g.row_relay(WD1)
-    g.row_rest(WD2)
-    o.up(half, half)
-    g.row_relay(WP)
-    p.first(D2)
-    g.row_rest(WP)
-    p.later(D2)
-    g.row_rest(WD1)
-    own_strips = p.branch()
+    p.hidden_grad()
+    p.mlp_strips()
     p.later(P1)
-    p.seq(D1)
-    p.seq_send(D1, 3)
     own_strips()
-    p.seq_send(D1, 2)
-    p.seq_send(D1, 1)
-    o.backward()
-    o.part_stage(c.fbits[0])
+    p.token_send(0, 3)
+    o.part_later()
     p.seq(D2)
     p.seq_send(D2, 3)
-    p.token_send(0, 3)
-    o.part_later()
+    p.first(U1)
     p.seq(P1)
     p.seq_send(D2, 2)
-    p.hidden_grad()
-    p.first(U1)
+    p.seq_send(D2, 1)
+    p.first(U2)
+    p.later(U2)
     p.seq_send(P1, 2)
-    p.first(U2)
+    p.token_send(0, 2)
     p.token_send(0, 1)
-    p.later(U1)
-    p.seq_send(D2, 1)
-    p.seq_send(P1, 3)
-    p.token_send(0, 2)
     o.part_home()
     p.norm_strips()
+    p.vec_begin()
     own_terms = p.input_strips()
-    p.first(Q1)
-    p.seq(U1)
-    p.seq_send(U1, 2)
-    p.seq_send(P1, 1)
     p.vec_fsdp()
-    own_terms()
-    p.vec_seq_start()
-    p.later(U2)
-    p.token_send(1, 3)
-    p.later(Q1)
-    p.seq_send(U1, 3)
+    p.seq_send(P1, 3)
     p.seq(U2)
     p.seq_send(U2, 2)
+    p.vec_seq_start()
+    p.later(U1)
+    p.seq_send(U2, 1)
+    own_terms()
+    p.first(Q1)
+    p.token_send(1, 3)
+    p.seq_send(U2, 3)
+    p.vec_seq_sum()
+    p.token_home(0)
+    p.later(Q1)
+    p.seq(U1)
+    p.seq_send(U1, 3)
     p.token_send(1, 2)
     p.token_send(1, 1)
     p.seq(Q1)
+    vec_home()
     p.seq_send(Q1, 2)
-    p.vec_seq_sum()
-    p.token_home(0)
     p.seq_send(U1, 1)
-    p.seq_send(U2, 1)
+    p.token_home(1)
     p.seq_send(Q1, 1)
-    p.seq_send(U2, 3)
+    p.seq_send(P1, 1)
     p.seq_send(Q1, 3)
-    vec_home()
-    p.token_home(1)
+    p.seq_send(U1, 2)
     p.seq_wait()
     p.home_wait()
     for i in range(len(vectors)):
@@ -1188,7 +1216,9 @@
     p.first(U1)
     p.first(U2)
     load("wu").wait()
+    p.mlp_strips()
     p.norm_strips()
+    p.vec_begin()
     p.seq(D1)
     p.seq_send(D1)
     p.later(Q1)
@@ -1262,7 +1292,7 @@
     if rows % LANES == 0 and (S, T, F) == (4, 2, 4):
         scratch = kept | passing | held | send_buffers(S, F, rows, ff, (P1, D1, D2)) | vectors
         scratch |= {k: (v.shape, v.dtype) for k, v in near.items()}
-        del scratch["row_info"]
+        del scratch["row_info"], scratch["row_sum"], scratch["acc"]
         sems = gather_sems | spread_sems | dict(near_sem=len(near), vec_sem=len(vectors))
         far |= {k + "_i": v for k, v in near.items()}
         outs |= {k + "_h": v for k, v in vectors.items()}

time: 224 us -> 222 us (level)
  no operation moved by 1% of the time
where the time goes in v2:
time: 222 us; the launch traced here: 219 us
  Pallas kernels  218 us (98%)
    pallas_call x1, Pallas kernels, launch(): pl.pallas_call(kernel, out_shape=[jax.ShapeDtypeStruct(*o) for o in [*out...  213 us
    pallas_call x1, Pallas kernels, finish(): pl.pallas_call(last_kernel, out_shape=outs, in_specs=[any_spec] * len(far...  5.14 us

profile of v2, /device:TPU:8, one launch (start us, length us, event | category | flops | bytes accessed | tf_op | source)
XLA Modules:
  0.0 218.7 jit_solution(10835944908552160464)
XLA Ops:
  0.7 212.7 %shard_map.263 = (bf16[128,1024]{1,0:T(8,128)(2,1)}, bf16[128,4096]{1,0:T(8,128)(2,1)}, bf16[128,3072]{1,0:T(8,128)(2,1)}, bf16[128,4096]{1,0:T(8,128)(2,1)}, f3...) custom-call(bf16[128,1024]{1,0:T(8,128)(2,1)} %refs_6_.1, ...), custom_call_target="tpu_custom_call" | custom-call | tf_op jit(solution)/shard_map/pallas_call | solution.py:912
  213.4 5.1 %shard_map.264 = (bf16[128,1024]{1,0:T(8,128)(2,1)}, bf16[128,1024]{1,0:T(8,128)(2,1)}, f32[1,2048]{1,0:T(1,128)}, f32[1,2048]{1,0:T(1,128)}, f32[1,2048]{1,0:T(...) custom-call(bf16[128,3072]{1,0:T(8,128)(2,1)} %get-tuple-element.38., ...), custom_call_target="tpu_custom_call" | custom-call | tf_op jit(solution)/shard_map/pallas_call | solution.py:1372

commit v3 on v2

--- a/solution.py
+++ b/solution.py
@@ -1325,9 +1325,20 @@
     sources, (gain, qkv_b, up_b, out_b, proj_bias, down_bias), refs = refs[:8], refs[8:14], refs[14:]
     outs, refs = refs[:14], refs[14:]
     held, wide, (hidden, norm, load_sem, out_sem) = refs[:8], refs[8:12], refs[12:]
-    loads = [pltpu.make_async_copy(a, b, load_sem.at[i]) for i, (a, b) in enumerate(zip(sources, held))]
-    for copy in loads:
-        copy.start()
+    loads = []
+
+    def load(src, dst):
+        loads.append(pltpu.make_async_copy(src, dst, load_sem.at[len(loads)]))
+        loads[-1].start()
+
+    rows = held[0].shape[0]
+    step = max(16, rows // 4)
+    parts = [slice(r, r + step) for r in range(0, rows, step)]
+    for i in range(4):
+        for part in parts:
+            load(sources[i].at[part, :], held[i].at[part, :])
+    for i in range(4, 8):
+        load(sources[i], held[i])
     stores = []
 
     def store(src, dst):
@@ -1340,14 +1351,11 @@
     for i, ref in enumerate((qkv_b, out_b, up_b, out_b)):
         store(ref, outs[7 + 2 * i])
     for i in range(4):
-        loads[i].wait()
-        rows = held[i].shape[0]
-        step = max(16, rows // 4)
-        for r in range(0, rows, step):
-            part = slice(r, r + step)
+        for r, part in enumerate(parts):
+            loads[i * len(parts) + r].wait()
             wide[i][part, :] = f32(held[i][part, :])
             store(wide[i].at[part, :], outs[6 + 2 * i].at[part, :])
-    for copy in loads[4:]:
+    for copy in loads[-4:]:
         copy.wait()
     hidden[...] = bf(f32(held[6][...]) + held[4][...] + proj_bias[...] + down_bias[...])
     norm[...] = bf(f32(held[7][...]) + held[5][...])
@@ -1377,7 +1385,7 @@
         scratch_shapes=[pltpu.VMEM(a.shape, a.dtype) for a in far]
         + [pltpu.VMEM(a.shape, WIDE) for a in far[:4]]
         + [pltpu.VMEM(hidden_in.shape, SMALL)] * 2
-        + [pltpu.SemaphoreType.DMA((len(far),)), pltpu.SemaphoreType.DMA((32,))],
+        + [pltpu.SemaphoreType.DMA((20,)), pltpu.SemaphoreType.DMA((32,))],
         compiler_params=pltpu.CompilerParams(vmem_limit_bytes=VMEM_BYTES),
     )(*far, *near)
     flat = {2, 3, 4, 5, 7, 9, 11, 13}

time: 222 us -> 223 us (level)
  no operation moved by 1% of the time
where the time goes in v3:
time: 223 us; the launch traced here: 220 us
  Pallas kernels  219 us (98%)
    pallas_call x1, Pallas kernels, launch(): pl.pallas_call(kernel, out_shape=[jax.ShapeDtypeStruct(*o) for o in [*out...  213 us
    pallas_call x1, Pallas kernels, finish(): pl.pallas_call(last_kernel, out_shape=outs, in_specs=[any_spec] * len(far...  5.94 us

profile of v3, /device:TPU:8, one launch (start us, length us, event | category | flops | bytes accessed | tf_op | source)
XLA Modules:
  0.0 219.5 jit_solution(4267094159856053968)
XLA Ops:
  0.7 212.7 %shard_map.263 = (bf16[128,1024]{1,0:T(8,128)(2,1)}, bf16[128,4096]{1,0:T(8,128)(2,1)}, bf16[128,3072]{1,0:T(8,128)(2,1)}, bf16[128,4096]{1,0:T(8,128)(2,1)}, f3...) custom-call(bf16[128,1024]{1,0:T(8,128)(2,1)} %refs_6_.1, ...), custom_call_target="tpu_custom_call" | custom-call | tf_op jit(solution)/shard_map/pallas_call | solution.py:912
  213.4 5.9 %shard_map.264 = (bf16[128,1024]{1,0:T(8,128)(2,1)}, bf16[128,1024]{1,0:T(8,128)(2,1)}, f32[1,2048]{1,0:T(1,128)}, f32[1,2048]{1,0:T(1,128)}, f32[1,2048]{1,0:T(...) custom-call(bf16[128,3072]{1,0:T(8,128)(2,1)} %get-tuple-element.38., ...), custom_call_target="tpu_custom_call" | custom-call | tf_op jit(solution)/shard_map/pallas_call | solution.py:1380
